TPU v7x, 16 devices: a whole 2x2x2 slice. The times are simulated.
16 devices in a mesh: data: 2 (over z), col: 2 (over y), row: 4 (over x, core).
Axes of the slice: x: 2, y: 2, z: 2, core: 2. Of those that a mesh axis runs over, the one named last changes fastest.
Arguments:
- x_in: bfloat16 [2048, 2048], P(None, 'row')
- h_act: bfloat16 [2048, 5632], P(None, 'row')
- d_gate: bfloat16 [2048, 5632], P(None, 'col')
- d_up: bfloat16 [2048, 5632], P(None, 'col')
- d_out: bfloat16 [2048, 2048], P(None, 'col')
- w_gate: float32 [2048, 5632], P('row', 'col')
- w_up: float32 [2048, 5632], P('row', 'col')
- w_down: float32 [5632, 2048], P('row', 'col')
- r_gate: float32 [2048], P('row')
- c_gate: float32 [5632], P('col')
- r_up: float32 [2048], P('row')
- c_up: float32 [5632], P('col')
- r_down: float32 [5632], P('row')
- c_down: float32 [2048], P('col')
- beta_two: float32 [], replicated
- rel_step: float32 [], replicated
- clip_thr: float32 [], replicated
Outputs:
- output 1: float32 [2048, 5632], P('row', 'col')
- output 2: float32 [2048, 5632], P('row', 'col')
- output 3: float32 [5632, 2048], P('row', 'col')
- output 4: float32 [2048], P('row')
- output 5: float32 [5632], P('col')
- output 6: float32 [2048], P('row')
- output 7: float32 [5632], P('col')
- output 8: float32 [5632], P('row')
- output 9: float32 [2048], P('col')
All inputs are finite; a program needn't handle non-finite values.
Results may differ from a plain program's by a relative error of at most 0.001.
Values are sent between devices in bfloat16 or wider.
A program may use at most 1 GiB of HBM per device.

v0:
```python
import jax
import jax.numpy as jnp
from jax import lax
from jax.sharding import PartitionSpec as P

EPS_SQ = 1e-30
EPS_SCALE = 1e-3
CONTRACT_TOKENS = (((0,), (0,)), ((), ()))


def solution(mesh):
    row_count = mesh.shape["row"]
    col_count = mesh.shape["col"]

    def block_step(w_blk, act_in, cot_out, r_old, c_old, beta_two, rel_step, clip_thr):
        g_blk = lax.dot_general(act_in, cot_out, CONTRACT_TOKENS, preferred_element_type=jnp.float32)
        m_total = g_blk.shape[0] * row_count
        n_total = g_blk.shape[1] * col_count
        q_blk = g_blk * g_blk + EPS_SQ
        row_sum = lax.psum(jnp.sum(q_blk, axis=1), "col")
        col_sum = lax.psum(jnp.sum(q_blk, axis=0), "row")
        r_new = beta_two * r_old + (1.0 - beta_two) * (row_sum / n_total)
        c_new = beta_two * c_old + (1.0 - beta_two) * (col_sum / m_total)
        r_mean = lax.psum(jnp.sum(r_new), "row") / m_total
        u_blk = g_blk / jnp.sqrt(r_new[:, None] * c_new[None, :] / r_mean)
        u_rms = jnp.sqrt(lax.psum(jnp.sum(u_blk * u_blk), ("row", "col")) / (m_total * n_total))
        w_rms = jnp.sqrt(lax.psum(jnp.sum(w_blk * w_blk), ("row", "col")) / (m_total * n_total))
        u_hat = u_blk / jnp.maximum(1.0, u_rms / clip_thr)
        step_size = rel_step * jnp.maximum(EPS_SCALE, w_rms)
        return w_blk - step_size * u_hat, r_new, c_new

    def local_program(x_in, h_act, d_gate, d_up, d_out, w_gate, w_up, w_down, r_gate, c_gate, r_up, c_up, r_down, c_down, beta_two, rel_step, clip_thr):
        gate_out = block_step(w_gate, x_in, d_gate, r_gate, c_gate, beta_two, rel_step, clip_thr)
        up_out = block_step(w_up, x_in, d_up, r_up, c_up, beta_two, rel_step, clip_thr)
        down_out = block_step(w_down, h_act, d_out, r_down, c_down, beta_two, rel_step, clip_thr)
        return (gate_out[0], up_out[0], down_out[0], gate_out[1], gate_out[2], up_out[1], up_out[2], down_out[1], down_out[2])

    act_spec = P(None, "row")
    cot_spec = P(None, "col")
    w_spec = P("row", "col")
    r_spec = P("row")
    c_spec = P("col")
    s_spec = P()
    return jax.shard_map(local_program, mesh=mesh, in_specs=(act_spec, act_spec, cot_spec, cot_spec, cot_spec, w_spec, w_spec, w_spec, r_spec, c_spec, r_spec, c_spec, r_spec, c_spec, s_spec, s_spec, s_spec), out_specs=(w_spec, w_spec, w_spec, r_spec, c_spec, r_spec, c_spec, r_spec, c_spec), check_vma=False)
```

profile of v0, /device:TPU:0, one launch (start us, length us, event | category | flops | bytes accessed | tf_op | source)
XLA Modules:
  0.0 114.5 jit_solution(12941866695308409526)
XLA Ops:
  0.6 0.0 copy-start
  2.8 0.0 copy-start.2
  2.8 0.0 copy-start.16
  2.8 0.0 copy-start.17
  2.8 4.9 %multiply_reduce_fusion.1 = f32[]{:T(128)} fusion(f32[1408,1024]{1,0:T(8,128)} %param.24), kind=kLoop, calls=%fused_computation.4 | loop fusion | flops 2883583 | bytes 5767172 | tf_op jit(solution)/shard_map/reduce_sum | solution.py:27
  7.7 0.0 copy-done.2
  7.7 0.0 slice-start.4
  7.7 0.0 slice-start.5
  7.7 5.6 %multiply_reduce_fusion.3 = (f32[]{:T(128)}, f32[]{:T(128)}) fusion(f32[512,2816]{1,0:T(8,128)} %param.23, f32[512,2816]{1,0:T(8,128)S(1)} %copy-done.2), kind=kLoop, calls=%fused_computation.9 | loop fusion | flops 5767166 | bytes 11534344 | tf_op jit(solution)/shard_map/reduce_sum | solution.py:27
  13.3 0.0 copy-done.16
  13.3 0.0 copy-done.17
  13.3 8.5 %fusion.4 = (f32[1024]{0:T(1024)S(1)}, f32[1408]{0:T(1024)S(1)}, f32[1408,1024]{1,0:T(8,128)}) fusion(bf16[2048,1408]{1,0:T(8,128)(2,1)S(1)} %copy-done.16, bf16[2048,1024]{1,0:T(8,128)(2,1)S(1)} %copy-done.17), kind=kOutput, calls=%fused_computation.19 | convolution fusion | flops 5911344640 | bytes 15738368 | tf_op jit(solution)/shard_map/dot_general | solution.py:16
  21.8 0.0 copy-done
  21.8 0.0 slice-done.4
  21.8 0.0 slice-done.5
  21.8 0.0 slice-done.6
  21.8 8.4 %fusion = (f32[2816]{0:T(1024)S(1)}, f32[512]{0:T(512)S(1)}, f32[512,2816]{1,0:T(8,128)}) fusion(bf16[2048,512]{1,0:T(8,128)(2,1)S(1)} %copy-done, bf16[2048,2816]{1,0:T(8,128)(2,1)S(1)} %bitcast.11), kind=kOutput, calls=%fused_computation.15 | convolution fusion | flops 5911343616 | bytes 19411968 | tf_op jit(solution)/shard_map/dot_general | solution.py:16
  30.2 0.0 copy-start.14
  30.2 0.0 copy-start.15
  30.2 0.0 copy-start.12
  30.2 0.0 copy-start.10
  30.2 11.5 %fusion.2 = (f32[2816]{0:T(1024)S(1)}, f32[512]{0:T(512)S(1)}, f32[512,2816]{1,0:T(8,128)}) fusion(bf16[2048,512]{1,0:T(8,128)(2,1)S(1)} %copy-done, bf16[2048,2816]{1,0:T(8,128)(2,1)} %param.20), kind=kOutput, calls=%fused_computation.17 | convolution fusion | flops 5911343616 | bytes 19411968 | tf_op jit(solution)/shard_map/dot_general | solution.py:16
  41.7 0.0 copy-start.13
  41.7 10.0 %all-reduce.2 = (f32[512]{0:T(512)S(1)}, f32[512]{0:T(512)S(1)}, f32[1408]{0:T(1024)S(1)}) all-reduce(f32[512]{0:T(512)S(1)} %get-tuple-element.14, f32[512]{0:T(512)S(1)} %get-tuple-element.12, f32[1408]{0:T(1024)S(1)} %get-tuple-element.10), channel_id=1, replica_groups=mesh['data'=2,'col'=2,'row'=4] {'col'}, use_global_device_ids=true, to_apply=%region_3.0 | all-reduce | flops 2432 | bytes 19456 | tf_op jit(solution)/shard_map/psum | solution.py:20
  51.7 0.0 copy-done.14
  51.7 0.0 copy-done.15
  51.7 0.6 fusion.7
  52.3 0.0 copy-start.9
  52.3 0.0 copy-start.8
  52.4 0.0 copy-done.12
  52.4 0.6 fusion.6
  53.0 0.0 copy-start.6
  53.0 11.5 %all-reduce.1 = (f32[]{:T(128)}, f32[2816]{0:T(1024)S(1)}, f32[]{:T(128)}, f32[2816]{0:T(1024)S(1)}, f32[]{:T(128)}, /*index=5*/f32[1024]{0:T(1024)S(1)}) all-reduce(f32[]{:T(128)} %get-tuple-element.39, f32[2816]{0:T(1024)S(1)} %get-tuple-element.13, f32[]{:T(128)} %get-tuple-element.32, ...), channel_id=1, replica_groups=mesh['data'=2,'col'=2,'row'=4] {'row'}, use_global_device_ids=true, to_apply=%region_7.0 | all-reduce | flops 6659 | bytes 53272 | tf_op jit(solution)/shard_map/psum | solution.py:24
  66.4 0.0 copy-done.10
  66.4 0.0 copy-start.4
  66.5 0.0 copy-start.11
  66.5 0.0 copy-start.3
  66.5 5.0 %multiply_reduce_fusion.4 = f32[]{:T(128)} fusion(f32[512,2816]{1,0:T(8,128)} %get-tuple-element.36, f32[]{:T(128)S(6)} %div.90, f32[2816]{0:T(1024)S(1)} %multiply_add_fusion.4, f32[512]{0:T(512)S(1)} %get-tuple-element.40), kind=kLoop, calls=%fused_computation.11 | loop fusion | flops 7208959 | bytes 5780488 | tf_op jit(solution)/shard_map/reduce_sum | solution.py:26
  71.4 0.0 copy-done.13
  71.4 0.0 copy-start.7
  71.4 4.9 %multiply_reduce_fusion = f32[]{:T(128)} fusion(f32[1408,1024]{1,0:T(8,128)} %get-tuple-element.38, f32[]{:T(128)S(6)} %div.108, f32[1024]{0:T(1024)S(1)} %multiply_add_fusion.6, f32[1408]{0:T(1024)S(1)} %get-tuple-element.31), kind=kLoop, calls=%fused_computation.1 | loop fusion | flops 7208959 | bytes 5776904 | tf_op jit(solution)/shard_map/reduce_sum | solution.py:26
  76.3 0.0 copy-done.11
  76.3 0.0 copy-done.3
  76.3 0.0 copy-start.5
  76.3 2.6 %multiply_reduce_fusion.2 = f32[]{:T(128)} fusion(f32[512,2816]{1,0:T(8,128)S(1)} %copy-done.3, f32[]{:T(128)S(6)} %div.99, f32[2816]{0:T(1024)S(1)} %multiply_add_fusion.3, f32[512]{0:T(512)S(1)} %get-tuple-element.33), kind=kLoop, calls=%fused_computation.6 | loop fusion | flops 7208959 | bytes 5780488 | tf_op jit(solution)/shard_map/reduce_sum | solution.py:26
  78.9 12.7 %all-reduce = (f32[]{:T(128)}, f32[]{:T(128)}, f32[]{:T(128)}, f32[]{:T(128)}, f32[]{:T(128)}, /*index=5*/f32[]{:T(128)}) all-reduce(f32[]{:T(128)} %multiply_reduce_fusion.4, f32[]{:T(128)} %get-tuple-element.42, f32[]{:T(128)} %multiply_reduce_fusion.2, ...), channel_id=1, replica_groups=mesh['data'=2,'col'=2,'row'=4] {'row','col'}, use_global_device_ids=true, to_apply=%region_9.0 | all-reduce | flops 6 | bytes 48 | tf_op jit(solution)/shard_map/psum | solution.py:26
  95.8 0.0 copy-done.9
  95.8 0.0 copy-done.4
  95.8 0.0 slice-start
  95.8 0.0 slice-start.2
  95.8 6.8 %multiply_subtract_fusion.2 = f32[512,2816]{1,0:T(8,128)} fusion(f32[512,2816]{1,0:T(8,128)} %param.22, f32[]{:T(128)S(6)} %max.19, f32[]{:T(128)S(6)} %mul.162, f32[512,2816]{1,0:T(8,128)} %get-tuple-element.36, f32[]{:T(128)S(6)} %div.90, f32[2816]{0:T(1024)S(1)} %multiply_add_fusion.4, f32[512]{0:T(512)S(1)} %get-tuple-element.40), kind=kLoop, calls=%fused_computation.10 | loop fusion | flops 8650752 | bytes 17314828 | tf_op jit(solution)/shard_map/sub | solution.py:30
  102.6 0.0 copy-done.8
  102.6 0.0 copy-done.5
  102.6 0.0 slice-start.3
  102.6 0.0 copy-start.1
  102.7 7.5 %multiply_subtract_fusion.1 = f32[512,2816]{1,0:T(8,128)} fusion(f32[512,2816]{1,0:T(8,128)} %param.23, f32[]{:T(128)S(6)} %max.21, f32[]{:T(128)S(6)} %mul.181, f32[512,2816]{1,0:T(8,128)} %get-tuple-element.37, f32[]{:T(128)S(6)} %div.99, f32[2816]{0:T(1024)S(1)} %multiply_add_fusion.3, f32[512]{0:T(512)S(1)} %get-tuple-element.33), kind=kLoop, calls=%fused_computation.5 | loop fusion | flops 8650752 | bytes 17314828 | tf_op jit(solution)/shard_map/sub | solution.py:30
  110.2 0.0 copy-done.6
  110.2 0.0 copy-done.7
  110.2 0.0 slice-done
  110.2 0.0 slice-done.2
  110.2 0.0 slice-done.1
  110.2 0.8 slice-done.3
  111.0 3.4 %multiply_subtract_fusion = f32[1408,1024]{1,0:T(8,128)} fusion(f32[1408,1024]{1,0:T(8,128)S(1)} %bitcast.7, f32[]{:T(128)S(6)} %max.23, f32[]{:T(128)S(6)} %mul.194, f32[1408,1024]{1,0:T(8,128)S(1)} %bitcast.9, f32[]{:T(128)S(6)} %div.108, f32[1024]{0:T(1024)S(1)} %multiply_add_fusion.6, f32[1408]{0:T(1024)S(1)} %get-tuple-element.31), kind=kLoop, calls=%fused_computation | loop fusion | flops 8650752 | bytes 17311244 | tf_op jit(solution)/shard_map/sub | solution.py:30
  114.5 0.0 copy-done.1
  (8 shorter events, 0.0 us)
Async XLA Ops:
  0.6 21.2 %copy-start = (bf16[2048,512]{1,0:T(8,128)(2,1)S(1)}, bf16[2048,512]{1,0:T(8,128)(2,1)}, u32[]{:S(2)}) copy-start(bf16[2048,512]{1,0:T(8,128)(2,1)} %param.17) | copy-start | bytes 6291460
  2.8 4.9 %copy-start.2 = (f32[512,2816]{1,0:T(8,128)S(1)}, f32[512,2816]{1,0:T(8,128)}, u32[]{:S(2)}) copy-start(f32[512,2816]{1,0:T(8,128)} %param.22) | copy-start | bytes 17301508
  2.8 10.5 %copy-start.16 = (bf16[2048,1408]{1,0:T(8,128)(2,1)S(1)}, bf16[2048,1408]{1,0:T(8,128)(2,1)}, u32[]{:S(2)}) copy-start(bf16[2048,1408]{1,0:T(8,128)(2,1)} %param.18) | copy-start | bytes 17301508
  2.8 10.5 %copy-start.17 = (bf16[2048,1024]{1,0:T(8,128)(2,1)S(1)}, bf16[2048,1024]{1,0:T(8,128)(2,1)}, u32[]{:S(2)}) copy-start(bf16[2048,1024]{1,0:T(8,128)(2,1)} %param.21) | copy-start | bytes 12582916
  7.7 14.1 %slice-start.4 = ((s8[11534336]{0:T(1024)(128)(4,1)}), s8[3145728]{0:T(1024)(128)(4,1)S(1)}, s32[]{:S(2)}) async-start(s8[11534336]{0:T(1024)(128)(4,1)} %bitcast.10), calls=%async_computation.4 | async-start | bytes 6291456
  7.7 14.1 %slice-start.5 = ((s8[11534336]{0:T(1024)(128)(4,1)}), s8[4194304]{0:T(1024)(128)(4,1)S(1)}, s32[]{:S(2)}) async-start(s8[11534336]{0:T(1024)(128)(4,1)} %bitcast.10), calls=%async_computation.5 | async-start | bytes 8388608
  13.3 8.5 %slice-start.6 = ((s8[11534336]{0:T(1024)(128)(4,1)}), s8[4194304]{0:T(1024)(128)(4,1)S(1)}, s32[]{:S(2)}) async-start(s8[11534336]{0:T(1024)(128)(4,1)} %bitcast.10), calls=%async_computation.6 | async-start | bytes 8388608
  30.2 21.5 %copy-start.14 = (f32[512]{0:T(512)S(1)}, f32[512]{0:T(512)}, u32[]{:S(2)}) copy-start(f32[512]{0:T(512)} %param.27) | copy-start | bytes 6148
  30.2 21.5 %copy-start.15 = (f32[512]{0:T(512)S(1)}, f32[512]{0:T(512)}, u32[]{:S(2)}) copy-start(f32[512]{0:T(512)} %param.25) | copy-start | bytes 6148
  30.2 22.1 %copy-start.12 = (f32[1408]{0:T(1024)S(1)}, f32[1408]{0:T(1024)}, u32[]{:S(2)}) copy-start(f32[1408]{0:T(1024)} %param.29) | copy-start | bytes 16900
  30.2 36.2 %copy-start.10 = (f32[2816]{0:T(1024)S(1)}, f32[2816]{0:T(1024)}, u32[]{:S(2)}) copy-start(f32[2816]{0:T(1024)} %param.26) | copy-start | bytes 33796
  41.7 29.7 %copy-start.13 = (f32[1024]{0:T(1024)S(1)}, f32[1024]{0:T(1024)}, u32[]{:S(2)}) copy-start(f32[1024]{0:T(1024)} %param.30) | copy-start | bytes 12292
  52.3 43.4 %copy-start.9 = (f32[512]{0:T(512)}, f32[512]{0:T(512)S(1)}, u32[]{:S(2)}) copy-start(f32[512]{0:T(512)S(1)} %get-tuple-element.40) | copy-start | bytes 6148
  52.3 50.3 %copy-start.8 = (f32[512]{0:T(512)}, f32[512]{0:T(512)S(1)}, u32[]{:S(2)}) copy-start(f32[512]{0:T(512)S(1)} %get-tuple-element.33) | copy-start | bytes 6148
  53.0 57.2 %copy-start.6 = (f32[1408]{0:T(1024)}, f32[1408]{0:T(1024)S(1)}, u32[]{:S(2)}) copy-start(f32[1408]{0:T(1024)S(1)} %get-tuple-element.31) | copy-start | bytes 16900
  66.4 29.3 %copy-start.4 = (f32[2816]{0:T(1024)}, f32[2816]{0:T(1024)S(1)}, u32[]{:S(2)}) copy-start(f32[2816]{0:T(1024)S(1)} %multiply_add_fusion.4) | copy-start | bytes 33796
  66.5 9.8 %copy-start.11 = (f32[2816]{0:T(1024)S(1)}, f32[2816]{0:T(1024)}, u32[]{:S(2)}) copy-start(f32[2816]{0:T(1024)} %param.28) | copy-start | bytes 33796
  66.5 9.8 %copy-start.3 = (f32[512,2816]{1,0:T(8,128)S(1)}, f32[512,2816]{1,0:T(8,128)}, u32[]{:S(2)}) copy-start(f32[512,2816]{1,0:T(8,128)} %get-tuple-element.37) | copy-start | bytes 17301508
  71.4 38.7 %copy-start.7 = (f32[1024]{0:T(1024)}, f32[1024]{0:T(1024)S(1)}, u32[]{:S(2)}) copy-start(f32[1024]{0:T(1024)S(1)} %multiply_add_fusion.6) | copy-start | bytes 12292
  76.3 26.3 %copy-start.5 = (f32[2816]{0:T(1024)}, f32[2816]{0:T(1024)S(1)}, u32[]{:S(2)}) copy-start(f32[2816]{0:T(1024)S(1)} %multiply_add_fusion.3) | copy-start | bytes 33796
  95.8 14.4 %slice-start = ((s8[5767168]{0:T(1024)(128)(4,1)}), s8[4194304]{0:T(1024)(128)(4,1)S(1)}, s32[]{:S(2)}) async-start(s8[5767168]{0:T(1024)(128)(4,1)} %bitcast.6), calls=%async_computation | async-start | bytes 8388608
  95.8 14.4 %slice-start.2 = ((s8[5767168]{0:T(1024)(128)(4,1)}), s8[4194304]{0:T(1024)(128)(4,1)S(1)}, s32[]{:S(2)}) async-start(s8[5767168]{0:T(1024)(128)(4,1)} %bitcast.8), calls=%async_computation.2 | async-start | bytes 8388608
  102.6 7.5 %slice-start.1 = ((s8[5767168]{0:T(1024)(128)(4,1)}), s8[1572864]{0:T(1024)(128)(4,1)S(1)}, s32[]{:S(2)}) async-start(s8[5767168]{0:T(1024)(128)(4,1)} %bitcast.6), calls=%async_computation.1 | async-start | bytes 3145728
  102.6 8.4 %slice-start.3 = ((s8[5767168]{0:T(1024)(128)(4,1)}), s8[1572864]{0:T(1024)(128)(4,1)S(1)}, s32[]{:S(2)}) async-start(s8[5767168]{0:T(1024)(128)(4,1)} %bitcast.8), calls=%async_computation.3 | async-start | bytes 3145728
  102.6 11.8 %copy-start.1 = (bf16[2048,512]{1,0:T(8,128)(2,1)S(1)}, bf16[2048,512]{1,0:T(8,128)(2,1)}, u32[]{:S(2)}) copy-start(bf16[2048,512]{1,0:T(8,128)(2,1)} %param.17) | copy-start | bytes 6291460
where the time goes:
time: 115 us; the launch traced here: 114 us
  other arithmetic  41.9 us (36%)
  blocking collectives  34.2 us (30%)
  matrix products  28.4 us (25%)
  between operations  9.06 us (8%)
    dot_general x3, matrix products, block_step(): lax.dot_general(act_in, cot_out, CONTRACT_TOKENS, preferred_element_type=...  28.4 us
    sub x3, other arithmetic, block_step(): return (w_blk - step_size * u_hat, r_new, c_new)  17.7 us
    psum x1, blocking collectives, block_step(): lax.psum(jnp.sum(u_blk * u_blk), ('row', 'col')) / (m_total * n_total)  12.7 us
    reduce_sum x3, other arithmetic, block_step(): jnp.sum(u_blk * u_blk)  12.4 us
    psum x1, blocking collectives, block_step(): r_mean = lax.psum(jnp.sum(r_new), 'row') / m_total  11.5 us
    reduce_sum x2, other arithmetic, block_step(): jnp.sum(w_blk * w_blk)  10.5 us
    psum x1, blocking collectives, block_step(): row_sum = lax.psum(jnp.sum(q_blk, axis=1), 'col')  10 us

commit v1 on v0

v1 whole, which is shorter than its diff:
```python
import jax
import jax.numpy as jnp
from jax import lax
from jax.experimental import pallas as pl
from jax.experimental.pallas import tpu as pltpu
from jax.sharding import PartitionSpec as P

EPS_SQ = 1e-30
EPS_SCALE = 1e-3
LANES = 128
K = 2048
ROWS, COLS = 4, 2
F32 = jnp.float32
BF16 = jnp.bfloat16
MESH = pl.DeviceIdType.MESH

SHAPES = ((512, 2816), (512, 2816), (1408, 1024))
TOTALS = tuple((m * ROWS, n * COLS) for m, n in SHAPES)
BLOCKS = (
    (0, 0, 1024), (0, 1024, 2048), (0, 2048, 2816),
    (1, 0, 1024), (1, 1024, 2048), (1, 2048, 2816),
    (2, 0, 512), (2, 512, 1024),
)
SLOTS = 3
SLOT_WIDTH = 1024
HCHUNK = 256
CHUNK = 64


def interleave(dots, units):
    done = 0
    for i, dot in enumerate(dots):
        dot()
        upto = len(units) * (i + 1) // len(dots)
        for unit in units[done:upto]:
            unit()
        done = upto
    for unit in units[done:]:
        unit()


def fold(x):
    return jnp.sum(x.reshape(x.shape[0] // 8, 8, x.shape[1]), axis=0)


def stats_kernel(
    x_hbm, h_hbm, dg_hbm, du_hbm, do_hbm, wg_hbm, wu_hbm, wd_hbm,
    rg, cg, ru, cu, rd, cd, beta, rel, clip,
    hg, hu, hd, wg, wu, wd, rg_new, cg_new, ru_new, cu_new, rd_new, cd_new, kap,
    ring, xs, xt, hs, ht, rowacc, abc_g, abc_u, abc_d, cacc_g, cacc_u, cacc_d,
    bv_g, bv_u, bv_d, rbuf_g, rbuf_u, rbuf_d, cbuf_g, cbuf_u, cbuf_d, sbuf, sacc, wacc,
    ring_sem, x_sem, h_sem, w_sem, r_send, r_recv, c_send, c_recv, s_send, s_recv,
):
    d_hbm = (dg_hbm, du_hbm, do_hbm)
    w_hbm = (wg_hbm, wu_hbm, wd_hbm)
    G = (hg, hu, hd)
    W = (wg, wu, wd)
    r_old, c_old = (rg, ru, rd), (cg, cu, cd)
    r_new, c_new = (rg_new, ru_new, rd_new), (cg_new, cu_new, cd_new)
    abc, cacc, bv = (abc_g, abc_u, abc_d), (cacc_g, cacc_u, cacc_d), (bv_g, bv_u, bv_d)
    rbuf, cbuf = (rbuf_g, rbuf_u, rbuf_d), (cbuf_g, cbuf_u, cbuf_d)

    me_d, me_c, me_r = lax.axis_index("data"), lax.axis_index("col"), lax.axis_index("row")
    me = me_c * ROWS + me_r

    def peer(dc, dr):
        return (me_d, lax.rem(me_c + dc, COLS), lax.rem(me_r + dr, ROWS))

    others = [(dc, dr) for dc in range(COLS) for dr in range(ROWS) if (dc, dr) != (0, 0)]

    def d_copy(j):
        mat, n0, n1 = BLOCKS[j]
        slot = j % SLOTS
        return pltpu.make_async_copy(
            d_hbm[mat].at[:, n0:n1], ring.at[slot, :, : n1 - n0], ring_sem.at[slot])

    XC = 4
    XK = K // XC

    def x_copy(c):
        return pltpu.make_async_copy(x_hbm.at[c * XK:(c + 1) * XK, :], xs.at[c * XK:(c + 1) * XK, :], x_sem.at[c])

    def d0_copy(c):
        n1 = BLOCKS[0][2]
        return pltpu.make_async_copy(
            dg_hbm.at[c * XK:(c + 1) * XK, 0:n1], ring.at[0, c * XK:(c + 1) * XK, 0:n1], x_sem.at[XC + c])

    HS = 4

    def h_copy(c):
        return pltpu.make_async_copy(h_hbm.at[c * HCHUNK:(c + 1) * HCHUNK, :], hs.at[c % HS], h_sem.at[c % HS])

    def w_copy(mat):
        return pltpu.make_async_copy(w_hbm[mat], W[mat], w_sem.at[mat])

    def row_copy(mat):
        return pltpu.make_async_remote_copy(
            src_ref=rbuf[mat].at[me_c], dst_ref=rbuf[mat].at[me_c],
            send_sem=r_send.at[mat], recv_sem=r_recv.at[mat],
            device_id=peer(1, 0), device_id_type=MESH)

    def col_copy(mat, d):
        return pltpu.make_async_remote_copy(
            src_ref=cbuf[mat].at[me_r], dst_ref=cbuf[mat].at[me_r],
            send_sem=c_send.at[mat, d - 1], recv_sem=c_recv.at[mat, d - 1],
            device_id=peer(0, d), device_id_type=MESH)

    def scal_copy(mat, i):
        return pltpu.make_async_remote_copy(
            src_ref=sbuf.at[mat, me], dst_ref=sbuf.at[mat, me],
            send_sem=s_send.at[mat, i], recv_sem=s_recv.at[mat, i],
            device_id=peer(*others[i]), device_id_type=MESH)

    def stats_units(j):
        mat, n0, n1 = BLOCKS[j]
        g_ref = G[mat]
        first = n0 == 0
        units = []
        for r in range(0, SHAPES[mat][0], CHUNK):
            def unit(r=r):
                part = None
                for t in range(n0 // LANES, n1 // LANES):
                    g = g_ref[r:r + CHUNK, t * LANES:(t + 1) * LANES]
                    q = g * g
                    part = q if part is None else part + q
                    col = fold(q)
                    cols = pl.ds(t * LANES, LANES)
                    cacc[mat][:, cols] = col if r == 0 else cacc[mat][:, cols] + col
                rows = pl.ds(r, CHUNK)
                rowacc[rows, :] = part if first else rowacc[rows, :] + part
            units.append(unit)
        return units

    def w2_units(mat):
        units = []
        m, n = SHAPES[mat]
        for r in range(0, m, CHUNK):
            def unit(r=r):
                acc = None
                for t in range(n // LANES):
                    w = W[mat][r:r + CHUNK, t * LANES:(t + 1) * LANES]
                    f = fold(w * w)
                    acc = f if acc is None else acc + f
                wacc[mat] = acc if r == 0 else wacc[mat] + acc
            units.append(unit)
        return units

    def scale_units(mat):
        units = []
        m, n = SHAPES[mat]
        for r in range(0, m, CHUNK):
            def unit(r=r):
                acc = None
                a = abc[mat][r:r + CHUNK, :]
                for t in range(n // LANES):
                    cols = slice(t * LANES, (t + 1) * LANES)
                    h = G[mat][r:r + CHUNK, cols] * a * bv[mat][t:t + 1, :]
                    G[mat][r:r + CHUNK, cols] = h
                    f = fold(h * h)
                    acc = f if acc is None else acc + f
                sacc[mat] = acc if r == 0 else sacc[mat] + acc
            units.append(unit)
        return units

    def transpose_units(c0, c1):
        units = []
        for c in range(c0, c1):
            for i in range(0, SHAPES[2][0], LANES):
                def unit(c=c, i=i):
                    ht[i:i + LANES, c * HCHUNK:(c + 1) * HCHUNK] = hs[c % HS, :, i:i + LANES].T
                units.append(unit)
        return units

    def send_sums(mat):
        m, n = SHAPES[mat]
        for i in range(m // LANES):
            block = rowacc[i * LANES:(i + 1) * LANES, :].T
            rbuf[mat][me_c, i:i + 1, :] = jnp.sum(block, axis=0, keepdims=True)
        for t in range(n // LANES):
            cbuf[mat][me_r, t:t + 1, :] = jnp.sum(
                cacc[mat][:, t * LANES:(t + 1) * LANES], axis=0, keepdims=True)
        row_copy(mat).start()
        for d in (1, 2, 3):
            col_copy(mat, d).start()

    def finish_sums(mat):
        m, n = SHAPES[mat]
        mt, nt = TOTALS[mat]
        row_copy(mat).wait_recv()
        for d in (1, 2, 3):
            col_copy(mat, d).wait_recv()
        b2 = beta[0]
        rows = rbuf[mat][0] + rbuf[mat][1]
        cols = (cbuf[mat][0] + cbuf[mat][1]) + (cbuf[mat][2] + cbuf[mat][3])
        rn = b2 * r_old[mat][...] + (1.0 - b2) * (rows * (1.0 / nt) + EPS_SQ)
        cn = b2 * c_old[mat][...] + (1.0 - b2) * (cols * (1.0 / mt) + EPS_SQ)
        r_new[mat][...] = rn
        c_new[mat][...] = cn
        a = lax.rsqrt(rn)
        bv[mat][...] = lax.rsqrt(cn)
        for i in range(m // LANES):
            abc[mat][i * LANES:(i + 1) * LANES, :] = jnp.broadcast_to(a[i:i + 1, :], (LANES, LANES)).T

    def send_scalars(mat):
        s = jnp.sum(sacc[mat], axis=0, keepdims=True)
        w = jnp.sum(wacc[mat], axis=0, keepdims=True)
        r = jnp.sum(r_new[mat][...], axis=0, keepdims=True)
        sbuf[mat, me] = jnp.concatenate([s, w, r, jnp.zeros((5, LANES), F32)], axis=0)
        for i in range(len(others)):
            scal_copy(mat, i).start()

    def finish_scalars(mat):
        mt, nt = TOTALS[mat]
        for i in range(len(others)):
            scal_copy(mat, i).wait_recv()
        tot = sbuf[mat, 0]
        for i in range(1, ROWS * COLS):
            tot = tot + sbuf[mat, i]
        tot = jnp.sum(tot, axis=1, keepdims=True)
        s, w, r = tot[0:1, :], tot[1:2, :], tot[2:3, :]
        r_mean = r * (1.0 / (COLS * mt))
        u_rms = jnp.sqrt(s * (1.0 / (mt * nt)) * r_mean)
        w_rms = jnp.sqrt(w * (1.0 / (mt * nt)))
        step = rel[0] * jnp.maximum(EPS_SCALE, w_rms)
        k = step * jnp.sqrt(r_mean) / jnp.maximum(1.0, u_rms / clip[0])
        kap[mat] = jnp.broadcast_to(k, (8, LANES))

    def dots_of(j):
        mat, n0, n1 = BLOCKS[j]
        slot = j % SLOTS
        lhs = ht if mat == 2 else xt
        m = SHAPES[mat][0]
        out = []

        def dot(r0, r1, c0, c1):
            def run():
                G[mat][r0:r1, n0 + c0:n0 + c1] = jnp.dot(
                    lhs[r0:r1, :], ring[slot, :, c0:c1], preferred_element_type=F32)
            return run

        mb = 352 if mat == 2 else 512
        w = n1 - n0
        for c in range(0, w, 512):
            if c + 512 <= w:
                out += [dot(r, r + mb, c, c + 512) for r in range(0, m, mb)]
            else:
                out += [dot(0, 256, c, w), dot(256, 512, c, w)]
        return out

    for c in range(XC):
        x_copy(c).start()
        d0_copy(c).start()
    d_copy(1).start()
    d_copy(2).start()

    barrier = pltpu.get_barrier_semaphore()
    for dc, dr in others:
        pl.semaphore_signal(barrier, inc=1, device_id=peer(dc, dr), device_id_type=MESH)

    for c in range(XC):
        x_copy(c).wait()
        d0_copy(c).wait()
        ks = slice(c * XK, (c + 1) * XK)
        for i in range(0, 512, LANES):
            xt[i:i + LANES, ks] = xs[ks, i:i + LANES].T
        for n in range(0, BLOCKS[0][2], 512):
            part = jnp.dot(xt[:, ks], ring[0, ks, n:n + 512], preferred_element_type=F32)
            hg[:, n:n + 512] = part if c == 0 else hg[:, n:n + 512] + part
    d_copy(3).start()
    for c in range(HS):
        h_copy(c).start()

    d_copy(1).wait()
    interleave(dots_of(1), stats_units(0))
    d_copy(4).start()
    w_copy(0).start()

    d_copy(2).wait()
    for c in (0, 1):
        h_copy(c).wait()
    interleave(dots_of(2), stats_units(1) + transpose_units(0, 2))
    d_copy(5).start()
    for c in (4, 5):
        h_copy(c).start()
    pl.semaphore_wait(barrier, len(others))

    d_copy(3).wait()
    for c in (2, 3):
        h_copy(c).wait()
    interleave(dots_of(3), stats_units(2) + transpose_units(2, 4))
    d_copy(6).start()
    for c in (6, 7):
        h_copy(c).start()
    w_copy(1).start()
    send_sums(0)

    d_copy(4).wait()
    for c in (4, 5):
        h_copy(c).wait()
    w_copy(0).wait()
    interleave(dots_of(4), stats_units(3) + transpose_units(4, 6) + w2_units(0))
    d_copy(7).start()
    w_copy(2).start()
    finish_sums(0)

    d_copy(5).wait()
    for c in (6, 7):
        h_copy(c).wait()
    interleave(dots_of(5), stats_units(4) + transpose_units(6, 8) + scale_units(0))
    send_scalars(0) if False else None

    d_copy(6).wait()
    w_copy(1).wait()
    interleave(dots_of(6), stats_units(5) + w2_units(1))
    send_scalars(0)
    send_sums(1)

    d_copy(7).wait()
    w_copy(2).wait()
    interleave(dots_of(7), stats_units(6) + w2_units(2))
    finish_scalars(0)
    for unit in stats_units(7):
        unit()
    send_sums(2)
    finish_sums(1)
    for unit in scale_units(1):
        unit()
    send_scalars(1)
    finish_sums(2)
    for unit in scale_units(2):
        unit()
    send_scalars(2)
    finish_scalars(1)
    finish_scalars(2)

    for mat in range(3):
        row_copy(mat).wait_send()
        for d in (1, 2, 3):
            col_copy(mat, d).wait_send()
        for i in range(len(others)):
            scal_copy(mat, i).wait_send()


def update_kernel(
    hg, hu, hd, wg, wu, wd, kap, rg, cg, ru, cu, rd, cd,
    og, ou, od, rg_o, cg_o, ru_o, cu_o, rd_o, cd_o,
    sg, su, sd, sems,
):
    H, W, O, S = (hg, hu, hd), (wg, wu, wd), (og, ou, od), (sg, su, sd)
    n_sem = 0
    copies = []
    for mat in range(3):
        m, n = SHAPES[mat]
        k = kap[mat][0:1, 0:1]
        step = 64 if mat < 2 else 128
        for r in range(0, m, step):
            for c in range(0, n, 256):
                S[mat][r:r + step, c:c + 256] = (
                    W[mat][r:r + step, c:c + 256] - k * H[mat][r:r + step, c:c + 256])
            copy = pltpu.make_async_copy(S[mat].at[r:r + step, :], O[mat].at[r:r + step, :], sems.at[n_sem])
            copy.start()
            copies.append(copy)
            n_sem += 1
    for src, dst in ((rg, rg_o), (cg, cg_o), (ru, ru_o), (cu, cu_o), (rd, rd_o), (cd, cd_o)):
        dst[...] = src[...]
    for copy in copies:
        copy.wait()


def local_program(x_in, h_act, d_gate, d_up, d_out, w_gate, w_up, w_down, r_gate, c_gate, r_up, c_up, r_down, c_down, beta_two, rel_step, clip_thr):
    any_spec = pl.BlockSpec(memory_space=pl.ANY)
    vmem_spec = pl.BlockSpec(memory_space=pltpu.VMEM)
    smem_spec = pl.BlockSpec(memory_space=pltpu.SMEM)
    stat_shapes = [(n // LANES, LANES) for shape in SHAPES for n in shape]
    stats = [v.reshape(s) for v, s in zip((r_gate, c_gate, r_up, c_up, r_down, c_down), stat_shapes)]
    scalars = [v.reshape(1) for v in (beta_two, rel_step, clip_thr)]
    big = [pltpu.HBM] * 8

    outs = pl.pallas_call(
        stats_kernel,
        out_shape=[pltpu.VMEM(s, F32) for s in SHAPES] * 2 + [pltpu.VMEM(s, F32) for s in stat_shapes]
        + [pltpu.VMEM((3, 8, LANES), F32)],
        in_specs=[any_spec] * 8 + [vmem_spec] * 6 + [smem_spec] * 3,
        out_specs=[vmem_spec] * 13,
        scratch_shapes=[
            pltpu.VMEM((SLOTS, K, SLOT_WIDTH), BF16),
            pltpu.VMEM((K, 512), BF16),
            pltpu.VMEM((512, K), BF16),
            pltpu.VMEM((4, HCHUNK, 1408), BF16),
            pltpu.VMEM((1408, K), BF16),
            pltpu.VMEM((1408, LANES), F32),
        ] + [pltpu.VMEM((m, LANES), F32) for m, n in SHAPES]
        + [pltpu.VMEM((8, n), F32) for m, n in SHAPES]
        + [pltpu.VMEM((n // LANES, LANES), F32) for m, n in SHAPES]
        + [pltpu.VMEM((COLS, m // LANES, LANES), F32) for m, n in SHAPES]
        + [pltpu.VMEM((ROWS, n // LANES, LANES), F32) for m, n in SHAPES]
        + [
            pltpu.VMEM((3, ROWS * COLS, 8, LANES), F32),
            pltpu.VMEM((3, 8, LANES), F32),
            pltpu.VMEM((3, 8, LANES), F32),
            pltpu.SemaphoreType.DMA((SLOTS,)),
            pltpu.SemaphoreType.DMA((8,)),
            pltpu.SemaphoreType.DMA((4,)),
            pltpu.SemaphoreType.DMA((3,)),
            pltpu.SemaphoreType.DMA((3,)),
            pltpu.SemaphoreType.DMA((3,)),
            pltpu.SemaphoreType.DMA((3, 3)),
            pltpu.SemaphoreType.DMA((3, 3)),
            pltpu.SemaphoreType.DMA((3, 7)),
            pltpu.SemaphoreType.DMA((3, 7)),
        ],
        compiler_params=pltpu.CompilerParams(
            collective_id=0, has_side_effects=True, vmem_limit_bytes=29 * 1024 * 1024),
        name="stats",
    )(
        *[pltpu.with_memory_space_constraint(v, pltpu.HBM)
          for v in (x_in, h_act, d_gate, d_up, d_out, w_gate, w_up, w_down)],
        *stats, *scalars)

    H, W, new, kap = outs[0:3], outs[3:6], outs[6:12], outs[12]
    res = pl.pallas_call(
        update_kernel,
        out_shape=[jax.ShapeDtypeStruct(s, F32) for s in SHAPES]
        + [jax.ShapeDtypeStruct(s, F32) for s in stat_shapes],
        in_specs=[vmem_spec] * 13,
        out_specs=[any_spec] * 3 + [vmem_spec] * 6,
        scratch_shapes=[pltpu.VMEM(s, F32) for s in SHAPES] + [pltpu.SemaphoreType.DMA((27,))],
        compiler_params=pltpu.CompilerParams(vmem_limit_bytes=29 * 1024 * 1024),
        name="update",
    )(*[pltpu.with_memory_space_constraint(v, pltpu.VMEM) for v in (*H, *W, kap, *new)])
    flat = [v.reshape(-1) for v in res[3:]]
    return (*res[:3], *flat)


def solution(mesh):
    act_spec = P(None, "row")
    cot_spec = P(None, "col")
    w_spec = P("row", "col")
    r_spec = P("row")
    c_spec = P("col")
    s_spec = P()
    return jax.shard_map(local_program, mesh=mesh, in_specs=(act_spec, act_spec, cot_spec, cot_spec, cot_spec, w_spec, w_spec, w_spec, r_spec, c_spec, r_spec, c_spec, r_spec, c_spec, s_spec, s_spec, s_spec), out_specs=(w_spec, w_spec, w_spec, r_spec, c_spec, r_spec, c_spec, r_spec, c_spec), check_vma=False)
```

time: 115 us -> 45.6 us (0.40)
  Pallas kernels: 0 us -> 42.6 us
  other arithmetic: 41.9 us -> 0 us
  blocking collectives: 34.2 us -> 0 us
  matrix products: 28.4 us -> 0 us
  between operations: 9.06 us -> 2.75 us
    pallas_call x0 -> x2, Pallas kernels: none -> 42.6 us  [the longest x1 35.7 us: local_program(): pl.pallas_call(stats_kernel, out_shape=[pltpu.VMEM(s, F32) for s in SHAPE...]
    psum x3 -> x0, blocking collectives: 34.2 us -> none  [the longest x1 12.7 us: block_step(): lax.psum(jnp.sum(u_blk * u_blk), ('row', 'col')) / (m_total * n_total)]
    dot_general x3 -> x0, matrix products: 28.4 us -> none  [block_step(): lax.dot_general(act_in, cot_out, CONTRACT_TOKENS, preferred_element_type=...]
    reduce_sum x7 -> x0, other arithmetic: 24.1 us -> none  [the longest x3 12.4 us: block_step(): jnp.sum(u_blk * u_blk)]
    sub x3 -> x0, other arithmetic: 17.7 us -> none  [block_step(): return (w_blk - step_size * u_hat, r_new, c_new)]
where the time goes in v1:
time: 45.6 us; the launch traced here: 45.4 us
  Pallas kernels  42.6 us (93%)
  between operations  2.75 us (6%)
    pallas_call x1, Pallas kernels, local_program(): pl.pallas_call(stats_kernel, out_shape=[pltpu.VMEM(s, F32) for s in SHAPE...  35.7 us
    pallas_call x1, Pallas kernels, local_program(): pl.pallas_call(update_kernel, out_shape=[jax.ShapeDtypeStruct(s, F32) for...  6.92 us

profile of v1, /device:TPU:0, one launch (start us, length us, event | category | flops | bytes accessed | tf_op | source)
XLA Modules:
  0.0 45.4 jit_solution(11879820409860319126)
XLA Ops:
  2.6 35.7 %stats.1 = (f32[512,2816]{1,0:T(8,128)S(1)}, f32[512,2816]{1,0:T(8,128)S(1)}, f32[1408,1024]{1,0:T(8,128)S(1)}, f32[512,2816]{1,0:T(8,128)S(1)}, f32[512,2816]{1...) custom-call(bf16[2048,512]{1,0:T(8,128)(2,1)} %x_hbm.1, ...), custom_call_target="tpu_custom_call" | custom-call | tf_op jit(solution)/shard_map/stats/pallas_call | solution.py:379
  38.3 6.9 %update.1 = (f32[512,2816]{1,0:T(8,128)}, f32[512,2816]{1,0:T(8,128)}, f32[1408,1024]{1,0:T(8,128)}, f32[4,128]{1,0:T(4,128)}, f32[22,128]{1,0:T(8,128)}, /*inde...) custom-call(f32[512,2816]{1,0:T(8,128)S(1)} %get-tuple-element.31.hg, ...), custom_call_target="tpu_custom_call" | custom-call | tf_op jit(solution)/shard_map/update/pallas_call | solution.py:421

commit v2 on v0

v2 whole, which is shorter than its diff:
```python
import jax
import jax.numpy as jnp
from jax import lax
from jax.experimental import pallas as pl
from jax.experimental.pallas import tpu as pltpu
from jax.sharding import PartitionSpec as P

EPS_SQ = 1e-30
EPS_SCALE = 1e-3
LANES = 128
K = 2048
ROWS, COLS = 4, 2
F32 = jnp.float32
BF16 = jnp.bfloat16
MESH = pl.DeviceIdType.MESH

DOWN, GATE, UP = 0, 1, 2
SHAPES = ((1408, 1024), (512, 2816), (512, 2816))
TOTALS = tuple((m * ROWS, n * COLS) for m, n in SHAPES)
PIECES = ((0, 256), (256, 512), (512, 1024), (1024, 1536), (1536, 2048))
GATE_BLOCKS = ((0, 1024), (1024, 2048), (2048, 2816))
UP_BLOCKS = ((0, 512), (512, 1536), (1536, 2048), (2048, 2816))
BLOCKS = tuple((GATE, *b) for b in GATE_BLOCKS) + tuple((UP, *b) for b in UP_BLOCKS)
SLOT_OF = (1, 2, 0, 1, 2, 0, 1)
CHUNK = 64
OTHERS = [(dc, dr) for dc in range(COLS) for dr in range(ROWS) if (dc, dr) != (0, 0)]


def interleave(dots, units):
    done = 0
    for i, dot in enumerate(dots):
        dot()
        upto = len(units) * (i + 1) // len(dots)
        for unit in units[done:upto]:
            unit()
        done = upto
    for unit in units[done:]:
        unit()


def fold(x):
    return jnp.sum(x.reshape(x.shape[0] // 8, 8, x.shape[1]), axis=0)


def place():
    return lax.axis_index("data"), lax.axis_index("col"), lax.axis_index("row")


def peer(dc, dr):
    d, c, r = place()
    return (d, lax.rem(c + dc, COLS), lax.rem(r + dr, ROWS))


def signal_entry(barrier):
    for dc, dr in OTHERS:
        pl.semaphore_signal(barrier, inc=1, device_id=peer(dc, dr), device_id_type=MESH)


def scalar_copies(buf, send, recv):
    _, c, r = place()
    me = c * ROWS + r
    return [
        pltpu.make_async_remote_copy(
            src_ref=buf.at[me], dst_ref=buf.at[me], send_sem=send.at[i], recv_sem=recv.at[i],
            device_id=peer(*OTHERS[i]), device_id_type=MESH)
        for i in range(len(OTHERS))
    ]


def scalar_tile(s, w, r):
    rows = [jnp.sum(v, axis=0, keepdims=True) for v in (s, w, r)]
    return jnp.concatenate(rows + [jnp.zeros((5, LANES), F32)], axis=0)


def step_of(mat, buf, rel, clip):
    mt, nt = TOTALS[mat]
    tot = buf[0]
    for i in range(1, ROWS * COLS):
        tot = tot + buf[i]
    tot = jnp.sum(tot, axis=1, keepdims=True)
    s, w, r = tot[0:1, :], tot[1:2, :], tot[2:3, :]
    r_mean = r * (1.0 / (COLS * mt))
    u_rms = jnp.sqrt(s * (1.0 / (mt * nt)) * r_mean)
    w_rms = jnp.sqrt(w * (1.0 / (mt * nt)))
    step = rel * jnp.maximum(EPS_SCALE, w_rms)
    k = step * jnp.sqrt(r_mean) / jnp.maximum(1.0, u_rms / clip)
    return jnp.broadcast_to(k, (8, LANES))


def main_kernel(
    x_hbm, h_hbm, dg_hbm, du_hbm, do_hbm, wg_hbm, wu_hbm, wd_hbm,
    rg, cg, ru, cu, rd, cd, beta, rel, clip,
    gu, wu, wd, wg, rd_new, cd_new, rg_new, cg_new, ru_new, cu_new, kap,
    gd, gg, ring, xt, hs, ht, rowacc, abc_d, abc_g, abc_u, cacc_d, cacc_g, cacc_u,
    bv_d, bv_g, bv_u, rbuf_d, rbuf_g, rbuf_u, cbuf_d, cbuf_g, cbuf_u, sbuf, sacc, wacc,
    ring_sem, h_sem, w_sem, r_send, r_recv, c_send, c_recv, s_send, s_recv,
):
    G, W = (gd, gg, gu), (wd, wg, wu)
    d_hbm, w_hbm = (do_hbm, dg_hbm, du_hbm), (wd_hbm, wg_hbm, wu_hbm)
    r_old, c_old = (rd, rg, ru), (cd, cg, cu)
    r_new, c_new = (rd_new, rg_new, ru_new), (cd_new, cg_new, cu_new)
    abc, cacc, bv = (abc_d, abc_g, abc_u), (cacc_d, cacc_g, cacc_u), (bv_d, bv_g, bv_u)
    rbuf, cbuf = (rbuf_d, rbuf_g, rbuf_u), (cbuf_d, cbuf_g, cbuf_u)
    _, me_c, me_r = place()

    def piece_copies(p):
        ks = slice(*PIECES[p])
        return (
            pltpu.make_async_copy(h_hbm.at[ks, :], hs.at[ks, :], h_sem.at[0, p]),
            pltpu.make_async_copy(do_hbm.at[ks, :], ring.at[0, ks, :], h_sem.at[1, p]),
        )

    x_copy = pltpu.make_async_copy(x_hbm, ring.at[2, :, :512], h_sem.at[2, 0])

    def d_copy(j):
        mat, n0, n1 = BLOCKS[j]
        slot = SLOT_OF[j]
        return pltpu.make_async_copy(
            d_hbm[mat].at[:, n0:n1], ring.at[slot, :, : n1 - n0], ring_sem.at[j])

    def w_copy(mat):
        return pltpu.make_async_copy(w_hbm[mat], W[mat], w_sem.at[mat])

    def sum_copies(mat):
        row = pltpu.make_async_remote_copy(
            src_ref=rbuf[mat].at[me_c], dst_ref=rbuf[mat].at[me_c],
            send_sem=r_send.at[mat], recv_sem=r_recv.at[mat],
            device_id=peer(1, 0), device_id_type=MESH)
        cols = [
            pltpu.make_async_remote_copy(
                src_ref=cbuf[mat].at[me_r], dst_ref=cbuf[mat].at[me_r],
                send_sem=c_send.at[mat, d - 1], recv_sem=c_recv.at[mat, d - 1],
                device_id=peer(0, d), device_id_type=MESH)
            for d in (1, 2, 3)
        ]
        return [row, *cols]

    def tiles(mat):
        return scalar_copies(sbuf.at[mat], s_send.at[mat], s_recv.at[mat])

    def start(copies):
        for c in copies:
            c.start()

    def wait(copies):
        for c in copies:
            c.wait()

    def wait_recv(copies):
        for c in copies:
            c.wait_recv()

    def stats_units(mat, n0, n1):
        units = []
        for r in range(0, SHAPES[mat][0], CHUNK):
            def unit(r=r):
                part = None
                for t in range(n0 // LANES, n1 // LANES):
                    g = G[mat][r:r + CHUNK, t * LANES:(t + 1) * LANES]
                    q = g * g
                    part = q if part is None else part + q
                    col = fold(q)
                    cols = pl.ds(t * LANES, LANES)
                    cacc[mat][:, cols] = col if r == 0 else cacc[mat][:, cols] + col
                rows = pl.ds(r, CHUNK)
                rowacc[rows, :] = part if n0 == 0 else rowacc[rows, :] + part
            units.append(unit)
        return units

    def sums_units(mat):
        m, n = SHAPES[mat]
        units = []
        for i in range(m // LANES):
            def rows(i=i):
                block = rowacc[i * LANES:(i + 1) * LANES, :].T
                rbuf[mat][me_c, i:i + 1, :] = jnp.sum(block, axis=0, keepdims=True)
            units.append(rows)
        for t in range(n // LANES):
            def cols(t=t):
                cbuf[mat][me_r, t:t + 1, :] = jnp.sum(
                    cacc[mat][:, t * LANES:(t + 1) * LANES], axis=0, keepdims=True)
            units.append(cols)
        return units

    def w2_units(mat):
        units = []
        m, n = SHAPES[mat]
        acc_ref = wacc.at[mat]
        for r in range(0, m, CHUNK):
            def unit(r=r):
                acc = None
                for t in range(n // LANES):
                    w = W[mat][r:r + CHUNK, t * LANES:(t + 1) * LANES]
                    f = fold(w * w)
                    acc = f if acc is None else acc + f
                acc_ref[...] = acc if r == 0 else acc_ref[...] + acc
            units.append(unit)
        return units

    def factor_units(mat):
        m, n = SHAPES[mat]
        mt, nt = TOTALS[mat]

        def new():
            b2 = beta[0]
            rows = rbuf[mat][0] + rbuf[mat][1]
            cols = (cbuf[mat][0] + cbuf[mat][1]) + (cbuf[mat][2] + cbuf[mat][3])
            rn = b2 * r_old[mat][...] + (1.0 - b2) * (rows * (1.0 / nt) + EPS_SQ)
            cn = b2 * c_old[mat][...] + (1.0 - b2) * (cols * (1.0 / mt) + EPS_SQ)
            r_new[mat][...] = rn
            c_new[mat][...] = cn
            bv[mat][...] = lax.rsqrt(cn)

        units = [new]
        for i in range(m // LANES):
            def unit(i=i):
                a = lax.rsqrt(r_new[mat][i:i + 1, :])
                abc[mat][i * LANES:(i + 1) * LANES, :] = jnp.broadcast_to(a, (LANES, LANES)).T
            units.append(unit)
        return units

    def scale_units(mat):
        units = []
        m, n = SHAPES[mat]
        for r in range(0, m, CHUNK):
            def unit(r=r):
                acc = None
                a = abc[mat][r:r + CHUNK, :]
                for t in range(n // LANES):
                    cols = slice(t * LANES, (t + 1) * LANES)
                    h = G[mat][r:r + CHUNK, cols] * a * bv[mat][t:t + 1, :]
                    G[mat][r:r + CHUNK, cols] = h
                    f = fold(h * h)
                    acc = f if acc is None else acc + f
                sacc[mat] = acc if r == 0 else sacc[mat] + acc
            units.append(unit)
        return units

    def update_units(mat):
        def step():
            kap[mat] = step_of(mat, sbuf.at[mat], rel[0], clip[0])

        units = [step]
        m, n = SHAPES[mat]
        for r in range(0, m, CHUNK):
            def unit(r=r):
                k = kap[mat, 0:1, :]
                for t in range(n // LANES):
                    cols = slice(t * LANES, (t + 1) * LANES)
                    W[mat][r:r + CHUNK, cols] = W[mat][r:r + CHUNK, cols] - k * G[mat][r:r + CHUNK, cols]
            units.append(unit)
        return units

    def tile_unit(mat):
        def unit():
            _, c, r = place()
            sbuf[mat, c * ROWS + r] = scalar_tile(sacc[mat], wacc[mat], r_new[mat][...])
        return [unit]

    def h_units(p):
        k0, k1 = PIECES[p]
        units = []
        for k in range(k0, k1, 256):
            for i in range(0, SHAPES[DOWN][0], LANES):
                def unit(k=k, i=i):
                    ht[i:i + LANES, k:k + 256] = hs[k:k + 256, i:i + LANES].T
                units.append(unit)
        return units

    def x_units():
        units = []
        for k in range(0, K, 256):
            for i in range(0, 512, LANES):
                def unit(k=k, i=i):
                    xt[i:i + LANES, k:k + 256] = ring[2, k:k + 256, i:i + LANES].T
                units.append(unit)
        return units

    def down_dots(p):
        ks = slice(*PIECES[p])
        out = []
        for r in range(0, 1408, 352):
            for c in range(0, 1024, 512):
                def dot(r=r, c=c):
                    rs, cs = slice(r, r + 352), slice(c, c + 512)
                    part = jnp.dot(ht[rs, ks], ring[0, ks, cs], preferred_element_type=F32)
                    gd[rs, cs] = part if p == 0 else gd[rs, cs] + part
                out.append(dot)
        return out

    def dots_of(j):
        mat, n0, n1 = BLOCKS[j]
        slot = SLOT_OF[j]
        out = []

        def dot(r0, r1, c0, c1):
            def run():
                G[mat][r0:r1, n0 + c0:n0 + c1] = jnp.dot(
                    xt[r0:r1, :], ring[slot, :, c0:c1], preferred_element_type=F32)
            return run

        w = n1 - n0
        for c in range(0, w, 512):
            if c + 512 <= w:
                out.append(dot(0, 512, c, c + 512))
            else:
                out += [dot(0, 256, c, w), dot(256, 512, c, w)]
        return out

    def run(units):
        for unit in units:
            unit()

    for p in (0, 1, 2):
        start(piece_copies(p))
    barrier = pltpu.get_barrier_semaphore()
    signal_entry(barrier)
    wait(piece_copies(0))
    start(piece_copies(3))
    start(piece_copies(4))
    x_copy.start()
    run(h_units(0))
    for p in range(4):
        wait(piece_copies(p + 1))
        if p == 2:
            d_copy(0).start()
            w_copy(DOWN).start()
        interleave(down_dots(p), h_units(p + 1))
    x_copy.wait()
    interleave(down_dots(4), x_units())
    d_copy(1).start()
    d_copy(2).start()

    d_copy(0).wait()
    interleave(dots_of(0), stats_units(DOWN, 0, 1024) + sums_units(DOWN))
    pl.semaphore_wait(barrier, len(OTHERS))
    start(sum_copies(DOWN))
    d_copy(3).start()
    w_copy(GATE).start()

    d_copy(1).wait()
    w_copy(DOWN).wait()
    interleave(dots_of(1), stats_units(GATE, 0, 1024) + w2_units(DOWN))
    d_copy(4).start()

    d_copy(2).wait()
    wait_recv(sum_copies(DOWN))
    interleave(dots_of(2), factor_units(DOWN) + scale_units(DOWN) + tile_unit(DOWN) + stats_units(GATE, 1024, 2048))
    start(tiles(DOWN))
    d_copy(5).start()
    w_copy(UP).start()

    d_copy(3).wait()
    interleave(dots_of(3), stats_units(GATE, 2048, 2816) + sums_units(GATE))
    start(sum_copies(GATE))
    d_copy(6).start()

    d_copy(4).wait()
    w_copy(GATE).wait()
    wait_recv(tiles(DOWN))
    interleave(dots_of(4), stats_units(UP, 0, 512) + w2_units(GATE) + update_units(DOWN)[:12])

    d_copy(5).wait()
    wait_recv(sum_copies(GATE))
    interleave(dots_of(5), factor_units(GATE) + scale_units(GATE) + tile_unit(GATE))
    start(tiles(GATE))

    d_copy(6).wait()
    w_copy(UP).wait()
    interleave(dots_of(6), update_units(DOWN)[12:] + stats_units(UP, 512, 1536) + stats_units(UP, 1536, 2048) + w2_units(UP))

    run(stats_units(UP, 2048, 2816) + sums_units(UP))
    start(sum_copies(UP))
    wait_recv(tiles(GATE))
    run(update_units(GATE))
    wait_recv(sum_copies(UP))
    run(factor_units(UP) + scale_units(UP) + tile_unit(UP))
    start(tiles(UP))
    for mat in range(3):
        for c in sum_copies(mat):
            c.wait_send()
    wait_recv(tiles(UP))
    kap[UP] = step_of(UP, sbuf.at[UP], rel[0], clip[0])
    for mat in range(3):
        for c in tiles(mat):
            c.wait_send()


def update_kernel(
    gu, wu, wd, wg, rd, cd, rg, cg, ru, cu, kap,
    wu_o, wd_o, wg_o, rd_o, cd_o, rg_o, cg_o, ru_o, cu_o, stage, sems, up_sems,
):
    srcs = (wd, wg, rd, cd, rg, cg, ru, cu)
    dsts = (wd_o, wg_o, rd_o, cd_o, rg_o, cg_o, ru_o, cu_o)
    copies = [pltpu.make_async_copy(src, dst, sems.at[i]) for i, (src, dst) in enumerate(zip(srcs, dsts))]
    for c in copies:
        c.start()
    m, n = SHAPES[UP]
    k = kap[UP, 0:1, :]
    for i, r in enumerate(range(0, m, CHUNK)):
        for t in range(n // LANES):
            cols = slice(t * LANES, (t + 1) * LANES)
            stage[r:r + CHUNK, cols] = wu[r:r + CHUNK, cols] - k * gu[r:r + CHUNK, cols]
        copies.append(pltpu.make_async_copy(stage.at[r:r + CHUNK, :], wu_o.at[r:r + CHUNK, :], up_sems.at[i]))
        copies[-1].start()
    for copy in copies:
        copy.wait()


VMEM_LIMIT = 41 * 1024 * 1024


def local_program(x_in, h_act, d_gate, d_up, d_out, w_gate, w_up, w_down, r_gate, c_gate, r_up, c_up, r_down, c_down, beta_two, rel_step, clip_thr):
    any_spec = pl.BlockSpec(memory_space=pl.ANY)
    vmem_spec = pl.BlockSpec(memory_space=pltpu.VMEM)
    smem_spec = pl.BlockSpec(memory_space=pltpu.SMEM)

    def stat_shape(v):
        return (v // LANES, LANES)

    stats = [v.reshape(stat_shape(v.shape[0])) for v in (r_gate, c_gate, r_up, c_up, r_down, c_down)]
    beta, rel, clip = [v.reshape(1) for v in (beta_two, rel_step, clip_thr)]
    rows = [stat_shape(m) for m, n in SHAPES]
    cols = [stat_shape(n) for m, n in SHAPES]
    dma = pltpu.SemaphoreType.DMA

    stat_pairs = [s for pair in zip(rows, cols) for s in pair]
    outs = pl.pallas_call(
        main_kernel,
        out_shape=[pltpu.VMEM(SHAPES[UP], F32)] * 2 + [pltpu.VMEM(s, F32) for s in SHAPES[:2]]
        + [pltpu.VMEM(s, F32) for s in stat_pairs] + [pltpu.VMEM((3, 8, LANES), F32)],
        in_specs=[any_spec] * 8 + [vmem_spec] * 6 + [smem_spec] * 3,
        out_specs=[vmem_spec] * 11,
        scratch_shapes=[
            pltpu.VMEM(SHAPES[DOWN], F32),
            pltpu.VMEM(SHAPES[GATE], F32),
            pltpu.VMEM((3, K, 1024), BF16),
            pltpu.VMEM((512, K), BF16),
            pltpu.VMEM((K, 1408), BF16),
            pltpu.VMEM((1408, K), BF16),
            pltpu.VMEM((1408, LANES), F32),
            pltpu.VMEM((1408, LANES), F32),
            pltpu.VMEM((512, LANES), F32),
            pltpu.VMEM((512, LANES), F32),
        ]
        + [pltpu.VMEM((8, n), F32) for m, n in SHAPES]
        + [pltpu.VMEM(s, F32) for s in cols]
        + [pltpu.VMEM((COLS, *s), F32) for s in rows]
        + [pltpu.VMEM((ROWS, *s), F32) for s in cols]
        + [
            pltpu.VMEM((3, ROWS * COLS, 8, LANES), F32),
            pltpu.VMEM((3, 8, LANES), F32),
            pltpu.VMEM((3, 8, LANES), F32),
            dma((7,)), dma((3, 5)), dma((3,)), dma((3,)), dma((3,)),
            dma((3, 3)), dma((3, 3)), dma((3, 7)), dma((3, 7)),
        ],
        compiler_params=pltpu.CompilerParams(
            collective_id=0, has_side_effects=True, vmem_limit_bytes=VMEM_LIMIT),
        name="main",
    )(
        *[pltpu.with_memory_space_constraint(v, pltpu.HBM)
          for v in (x_in, h_act, d_gate, d_up, d_out, w_gate, w_up, w_down)],
        *stats, beta, rel, clip)
    held = [pltpu.with_memory_space_constraint(v, pltpu.VMEM) for v in outs]
    res = pl.pallas_call(
        update_kernel,
        out_shape=[jax.ShapeDtypeStruct(s, F32) for s in (SHAPES[UP], *SHAPES[:2], *stat_pairs)],
        in_specs=[vmem_spec] * 11,
        out_specs=[any_spec] * 9,
        scratch_shapes=[pltpu.VMEM(SHAPES[UP], F32), dma((8,)), dma((8,))],
        compiler_params=pltpu.CompilerParams(vmem_limit_bytes=VMEM_LIMIT),
        name="update",
    )(*held)
    up, down, gate, rd_n, cd_n, rg_n, cg_n, ru_n, cu_n = res
    flat = [v.reshape(-1) for v in (rg_n, cg_n, ru_n, cu_n, rd_n, cd_n)]
    return (gate, up, down, *flat)


def solution(mesh):
    act_spec = P(None, "row")
    cot_spec = P(None, "col")
    w_spec = P("row", "col")
    r_spec = P("row")
    c_spec = P("col")
    s_spec = P()
    return jax.shard_map(local_program, mesh=mesh, in_specs=(act_spec, act_spec, cot_spec, cot_spec, cot_spec, w_spec, w_spec, w_spec, r_spec, c_spec, r_spec, c_spec, r_spec, c_spec, s_spec, s_spec, s_spec), out_specs=(w_spec, w_spec, w_spec, r_spec, c_spec, r_spec, c_spec, r_spec, c_spec), check_vma=False)
```

time: 115 us -> 47.7 us (0.41)
  Pallas kernels: 0 us -> 44.7 us
  other arithmetic: 41.9 us -> 0 us
  blocking collectives: 34.2 us -> 0 us
  matrix products: 28.4 us -> 0 us
  between operations: 9.06 us -> 2.75 us
    pallas_call x0 -> x2, Pallas kernels: none -> 44.7 us  [the longest x1 38.4 us: local_program(): pl.pallas_call(main_kernel, out_shape=[pltpu.VMEM(SHAPES[UP], F32)] * 2 +...]
    psum x3 -> x0, blocking collectives: 34.2 us -> none  [the longest x1 12.7 us: block_step(): lax.psum(jnp.sum(u_blk * u_blk), ('row', 'col')) / (m_total * n_total)]
    dot_general x3 -> x0, matrix products: 28.4 us -> none  [block_step(): lax.dot_general(act_in, cot_out, CONTRACT_TOKENS, preferred_element_type=...]
    reduce_sum x7 -> x0, other arithmetic: 24.1 us -> none  [the longest x3 12.4 us: block_step(): jnp.sum(u_blk * u_blk)]
    sub x3 -> x0, other arithmetic: 17.7 us -> none  [block_step(): return (w_blk - step_size * u_hat, r_new, c_new)]
where the time goes in v2:
time: 47.7 us; the launch traced here: 47.5 us
  Pallas kernels  44.7 us (94%)
  between operations  2.75 us (6%)
    pallas_call x1, Pallas kernels, local_program(): pl.pallas_call(main_kernel, out_shape=[pltpu.VMEM(SHAPES[UP], F32)] * 2 +...  38.4 us
    pallas_call x1, Pallas kernels, local_program(): pl.pallas_call(update_kernel, out_shape=[jax.ShapeDtypeStruct(s, F32) for...  6.29 us

profile of v2, /device:TPU:0, one launch (start us, length us, event | category | flops | bytes accessed | tf_op | source)
XLA Modules:
  0.0 47.5 jit_solution(4837232117561790308)
XLA Ops:
  2.6 38.4 %main.1 = (f32[512,2816]{1,0:T(8,128)S(1)}, f32[512,2816]{1,0:T(8,128)S(1)}, f32[1408,1024]{1,0:T(8,128)S(1)}, f32[512,2816]{1,0:T(8,128)S(1)}, f32[11,128]{1,0:...) custom-call(bf16[2048,512]{1,0:T(8,128)(2,1)} %x_hbm.1, ...), custom_call_target="tpu_custom_call" | custom-call | tf_op jit(solution)/shard_map/main/pallas_call | solution.py:428
  41.0 6.3 %update.1 = (f32[512,2816]{1,0:T(8,128)}, f32[1408,1024]{1,0:T(8,128)}, f32[512,2816]{1,0:T(8,128)}, f32[11,128]{1,0:T(8,128)}, f32[8,128]{1,0:T(8,128)}, /*inde...) custom-call(f32[512,2816]{1,0:T(8,128)S(1)} %get-tuple-element.29.gu, ...), custom_call_target="tpu_custom_call" | custom-call | tf_op jit(solution)/shard_map/update/pallas_call | solution.py:465

commit v3 on v2

--- a/solution.py
+++ b/solution.py
@@ -21,7 +21,7 @@
 GATE_BLOCKS = ((0, 1024), (1024, 2048), (2048, 2816))
 UP_BLOCKS = ((0, 512), (512, 1536), (1536, 2048), (2048, 2816))
 BLOCKS = tuple((GATE, *b) for b in GATE_BLOCKS) + tuple((UP, *b) for b in UP_BLOCKS)
-SLOT_OF = (1, 2, 0, 1, 2, 0, 1)
+EARLY_COLS = 16
 CHUNK = 64
 OTHERS = [(dc, dr) for dc in range(COLS) for dr in range(ROWS) if (dc, dr) != (0, 0)]
 
@@ -29,13 +29,11 @@
 def interleave(dots, units):
     done = 0
     for i, dot in enumerate(dots):
-        dot()
         upto = len(units) * (i + 1) // len(dots)
         for unit in units[done:upto]:
             unit()
         done = upto
-    for unit in units[done:]:
-        unit()
+        dot()
 
 
 def fold(x):
@@ -89,11 +87,11 @@
 
 def main_kernel(
     x_hbm, h_hbm, dg_hbm, du_hbm, do_hbm, wg_hbm, wu_hbm, wd_hbm,
-    rg, cg, ru, cu, rd, cd, beta, rel, clip,
-    gu, wu, wd, wg, rd_new, cd_new, rg_new, cg_new, ru_new, cu_new, kap,
-    gd, gg, ring, xt, hs, ht, rowacc, abc_d, abc_g, abc_u, cacc_d, cacc_g, cacc_u,
-    bv_d, bv_g, bv_u, rbuf_d, rbuf_g, rbuf_u, cbuf_d, cbuf_g, cbuf_u, sbuf, sacc, wacc,
-    ring_sem, h_sem, w_sem, r_send, r_recv, c_send, c_recv, s_send, s_recv,
+    rg_hbm, cg_hbm, ru_hbm, cu_hbm, rd_hbm, cd_hbm, beta, rel, clip,
+    gu, wu, wd, wg, rd_new, cd_new, rg_new, cg_new, ru_new, cu_new, kap, abc_u, bv_u,
+    gd, gg, ring, xt, hs, ht, rowacc, abc_d, abc_g, cacc_d, cacc_g, cacc_u,
+    bv_d, bv_g, rd, cd, rg, cg, ru, cu, rbuf_d, rbuf_g, rbuf_u, cbuf_d, cbuf_g, cbuf_u, sbuf, sacc, wacc,
+    ring_sem, h_sem, w_sem, old_sem, r_send, r_recv, c_send, c_recv, s_send, s_recv,
 ):
     G, W = (gd, gg, gu), (wd, wg, wu)
     d_hbm, w_hbm = (do_hbm, dg_hbm, du_hbm), (wd_hbm, wg_hbm, wu_hbm)
@@ -112,28 +110,40 @@
 
     x_copy = pltpu.make_async_copy(x_hbm, ring.at[2, :, :512], h_sem.at[2, 0])
 
+    places = (
+        ring.at[1], hs.at[:, :1024], ring.at[2, :, :768],
+        ring.at[0, :, :512], ring.at[1], ring.at[0, :, 512:1024], hs.at[:, :768],
+    )
+
     def d_copy(j):
         mat, n0, n1 = BLOCKS[j]
-        slot = SLOT_OF[j]
-        return pltpu.make_async_copy(
-            d_hbm[mat].at[:, n0:n1], ring.at[slot, :, : n1 - n0], ring_sem.at[j])
+        return pltpu.make_async_copy(d_hbm[mat].at[:, n0:n1], places[j], ring_sem.at[j])
+
+    old_copies = [
+        pltpu.make_async_copy(src, dst, old_sem.at[i])
+        for i, (src, dst) in enumerate(zip((rd_hbm, cd_hbm, rg_hbm, cg_hbm, ru_hbm, cu_hbm), (rd, cd, rg, cg, ru, cu)))
+    ]
 
     def w_copy(mat):
         return pltpu.make_async_copy(w_hbm[mat], W[mat], w_sem.at[mat])
+
+    def col_copies(mat, part, sem):
+        return [
+            pltpu.make_async_remote_copy(
+                src_ref=cbuf[mat].at[me_r, part], dst_ref=cbuf[mat].at[me_r, part],
+                send_sem=c_send.at[sem, d - 1], recv_sem=c_recv.at[sem, d - 1],
+                device_id=peer(0, d), device_id_type=MESH)
+            for d in (1, 2, 3)
+        ]
+
+    early = col_copies(UP, slice(0, EARLY_COLS), 3)
 
     def sum_copies(mat):
         row = pltpu.make_async_remote_copy(
             src_ref=rbuf[mat].at[me_c], dst_ref=rbuf[mat].at[me_c],
             send_sem=r_send.at[mat], recv_sem=r_recv.at[mat],
             device_id=peer(1, 0), device_id_type=MESH)
-        cols = [
-            pltpu.make_async_remote_copy(
-                src_ref=cbuf[mat].at[me_r], dst_ref=cbuf[mat].at[me_r],
-                send_sem=c_send.at[mat, d - 1], recv_sem=c_recv.at[mat, d - 1],
-                device_id=peer(0, d), device_id_type=MESH)
-            for d in (1, 2, 3)
-        ]
-        return [row, *cols]
+        return [row, *col_copies(mat, slice(EARLY_COLS if mat == UP else 0, SHAPES[mat][1] // LANES), mat)]
 
     def tiles(mat):
         return scalar_copies(sbuf.at[mat], s_send.at[mat], s_recv.at[mat])
@@ -167,33 +177,38 @@
             units.append(unit)
         return units
 
-    def sums_units(mat):
-        m, n = SHAPES[mat]
-        units = []
-        for i in range(m // LANES):
+    def row_units(mat):
+        units = []
+        for i in range(SHAPES[mat][0] // LANES):
             def rows(i=i):
                 block = rowacc[i * LANES:(i + 1) * LANES, :].T
                 rbuf[mat][me_c, i:i + 1, :] = jnp.sum(block, axis=0, keepdims=True)
             units.append(rows)
-        for t in range(n // LANES):
+        return units
+
+    def col_units(mat, t0, t1):
+        units = []
+        for t in range(t0, t1):
             def cols(t=t):
                 cbuf[mat][me_r, t:t + 1, :] = jnp.sum(
                     cacc[mat][:, t * LANES:(t + 1) * LANES], axis=0, keepdims=True)
             units.append(cols)
         return units
 
+    def sums_units(mat):
+        return row_units(mat) + col_units(mat, 0, SHAPES[mat][1] // LANES)
+
     def w2_units(mat):
         units = []
         m, n = SHAPES[mat]
-        acc_ref = wacc.at[mat]
-        for r in range(0, m, CHUNK):
-            def unit(r=r):
+        for i in range(m // CHUNK):
+            def unit(i=i):
                 acc = None
                 for t in range(n // LANES):
-                    w = W[mat][r:r + CHUNK, t * LANES:(t + 1) * LANES]
+                    w = W[mat][i * CHUNK:(i + 1) * CHUNK, t * LANES:(t + 1) * LANES]
                     f = fold(w * w)
                     acc = f if acc is None else acc + f
-                acc_ref[...] = acc if r == 0 else acc_ref[...] + acc
+                wacc[mat, i] = acc
             units.append(unit)
         return units
 
@@ -222,17 +237,16 @@
     def scale_units(mat):
         units = []
         m, n = SHAPES[mat]
-        for r in range(0, m, CHUNK):
-            def unit(r=r):
+        for i in range(m // CHUNK):
+            def unit(i=i):
                 acc = None
-                a = abc[mat][r:r + CHUNK, :]
+                rows = slice(i * CHUNK, (i + 1) * CHUNK)
+                a = abc[mat][rows, :]
                 for t in range(n // LANES):
-                    cols = slice(t * LANES, (t + 1) * LANES)
-                    h = G[mat][r:r + CHUNK, cols] * a * bv[mat][t:t + 1, :]
-                    G[mat][r:r + CHUNK, cols] = h
+                    h = G[mat][rows, t * LANES:(t + 1) * LANES] * a * bv[mat][t:t + 1, :]
                     f = fold(h * h)
                     acc = f if acc is None else acc + f
-                sacc[mat] = acc if r == 0 else sacc[mat] + acc
+                sacc[mat, i] = acc
             units.append(unit)
         return units
 
@@ -244,17 +258,20 @@
         m, n = SHAPES[mat]
         for r in range(0, m, CHUNK):
             def unit(r=r):
-                k = kap[mat, 0:1, :]
+                ka = abc[mat][r:r + CHUNK, :] * kap[mat, 0:1, :]
                 for t in range(n // LANES):
                     cols = slice(t * LANES, (t + 1) * LANES)
-                    W[mat][r:r + CHUNK, cols] = W[mat][r:r + CHUNK, cols] - k * G[mat][r:r + CHUNK, cols]
+                    W[mat][r:r + CHUNK, cols] = (
+                        W[mat][r:r + CHUNK, cols] - G[mat][r:r + CHUNK, cols] * ka * bv[mat][t:t + 1, :])
             units.append(unit)
         return units
 
     def tile_unit(mat):
         def unit():
             _, c, r = place()
-            sbuf[mat, c * ROWS + r] = scalar_tile(sacc[mat], wacc[mat], r_new[mat][...])
+            chunks = SHAPES[mat][0] // CHUNK
+            sbuf[mat, c * ROWS + r] = scalar_tile(
+                jnp.sum(sacc[mat, :chunks], axis=0), jnp.sum(wacc[mat, :chunks], axis=0), r_new[mat][...])
         return [unit]
 
     def h_units(p):
@@ -290,13 +307,12 @@
 
     def dots_of(j):
         mat, n0, n1 = BLOCKS[j]
-        slot = SLOT_OF[j]
         out = []
 
         def dot(r0, r1, c0, c1):
             def run():
                 G[mat][r0:r1, n0 + c0:n0 + c1] = jnp.dot(
-                    xt[r0:r1, :], ring[slot, :, c0:c1], preferred_element_type=F32)
+                    xt[r0:r1, :], places[j][:, c0:c1], preferred_element_type=F32)
             return run
 
         w = n1 - n0
@@ -313,6 +329,7 @@
 
     for p in (0, 1, 2):
         start(piece_copies(p))
+    start(old_copies)
     barrier = pltpu.get_barrier_semaphore()
     signal_entry(barrier)
     wait(piece_copies(0))
@@ -322,72 +339,75 @@
     run(h_units(0))
     for p in range(4):
         wait(piece_copies(p + 1))
-        if p == 2:
+        if p == 1:
             d_copy(0).start()
-            w_copy(DOWN).start()
         interleave(down_dots(p), h_units(p + 1))
+    d_copy(1).start()
     x_copy.wait()
     interleave(down_dots(4), x_units())
-    d_copy(1).start()
     d_copy(2).start()
+    w_copy(DOWN).start()
+    d_copy(3).start()
+    d_copy(5).start()
 
     d_copy(0).wait()
+    wait(old_copies)
     interleave(dots_of(0), stats_units(DOWN, 0, 1024) + sums_units(DOWN))
     pl.semaphore_wait(barrier, len(OTHERS))
     start(sum_copies(DOWN))
-    d_copy(3).start()
+    d_copy(4).start()
     w_copy(GATE).start()
 
     d_copy(1).wait()
+    d_copy(2).wait()
     w_copy(DOWN).wait()
-    interleave(dots_of(1), stats_units(GATE, 0, 1024) + w2_units(DOWN))
-    d_copy(4).start()
-
-    d_copy(2).wait()
-    wait_recv(sum_copies(DOWN))
-    interleave(dots_of(2), factor_units(DOWN) + scale_units(DOWN) + tile_unit(DOWN) + stats_units(GATE, 1024, 2048))
-    start(tiles(DOWN))
-    d_copy(5).start()
+    interleave(dots_of(1), stats_units(GATE, 0, 1024) + w2_units(DOWN)[:11])
+    interleave(dots_of(2), w2_units(DOWN)[11:] + stats_units(GATE, 1024, 2048))
+    d_copy(6).start()
     w_copy(UP).start()
 
     d_copy(3).wait()
     interleave(dots_of(3), stats_units(GATE, 2048, 2816) + sums_units(GATE))
     start(sum_copies(GATE))
-    d_copy(6).start()
 
     d_copy(4).wait()
+    d_copy(5).wait()
     w_copy(GATE).wait()
+    wait_recv(sum_copies(DOWN))
+    interleave(dots_of(4), factor_units(DOWN) + scale_units(DOWN) + stats_units(UP, 0, 512))
+    interleave(dots_of(5), tile_unit(DOWN) + w2_units(GATE) + stats_units(UP, 512, 1536))
+    start(tiles(DOWN))
+
+    d_copy(6).wait()
+    wait_recv(sum_copies(GATE))
+    interleave(
+        dots_of(6),
+        factor_units(GATE) + scale_units(GATE) + tile_unit(GATE) + stats_units(UP, 1536, 2048)
+        + col_units(UP, 0, EARLY_COLS))
+    start(tiles(GATE))
+    start(early)
+
+    run(stats_units(UP, 2048, 2816) + row_units(UP) + col_units(UP, EARLY_COLS, 22))
+    start(sum_copies(UP))
+    w_copy(UP).wait()
+    run(w2_units(UP))
     wait_recv(tiles(DOWN))
-    interleave(dots_of(4), stats_units(UP, 0, 512) + w2_units(GATE) + update_units(DOWN)[:12])
-
-    d_copy(5).wait()
-    wait_recv(sum_copies(GATE))
-    interleave(dots_of(5), factor_units(GATE) + scale_units(GATE) + tile_unit(GATE))
-    start(tiles(GATE))
-
-    d_copy(6).wait()
-    w_copy(UP).wait()
-    interleave(dots_of(6), update_units(DOWN)[12:] + stats_units(UP, 512, 1536) + stats_units(UP, 1536, 2048) + w2_units(UP))
-
-    run(stats_units(UP, 2048, 2816) + sums_units(UP))
-    start(sum_copies(UP))
-    wait_recv(tiles(GATE))
-    run(update_units(GATE))
+    run(update_units(DOWN))
+    wait_recv(early)
     wait_recv(sum_copies(UP))
     run(factor_units(UP) + scale_units(UP) + tile_unit(UP))
     start(tiles(UP))
-    for mat in range(3):
-        for c in sum_copies(mat):
+    wait_recv(tiles(GATE))
+    run(update_units(GATE))
+    for copies in [sum_copies(mat) for mat in range(3)] + [early, tiles(DOWN), tiles(GATE), tiles(UP)]:
+        for c in copies:
             c.wait_send()
     wait_recv(tiles(UP))
     kap[UP] = step_of(UP, sbuf.at[UP], rel[0], clip[0])
-    for mat in range(3):
-        for c in tiles(mat):
-            c.wait_send()
 
 
 def update_kernel(
-    gu, wu, wd, wg, rd, cd, rg, cg, ru, cu, kap,
+    gu, wu, wd, wg, rd, cd, rg, cg, ru, cu, kap, abc, bv,
     wu_o, wd_o, wg_o, rd_o, cd_o, rg_o, cg_o, ru_o, cu_o, stage, sems, up_sems,
 ):
     srcs = (wd, wg, rd, cd, rg, cg, ru, cu)
@@ -398,9 +418,10 @@
     m, n = SHAPES[UP]
     k = kap[UP, 0:1, :]
     for i, r in enumerate(range(0, m, CHUNK)):
+        ka = abc[r:r + CHUNK, :] * k
         for t in range(n // LANES):
             cols = slice(t * LANES, (t + 1) * LANES)
-            stage[r:r + CHUNK, cols] = wu[r:r + CHUNK, cols] - k * gu[r:r + CHUNK, cols]
+            stage[r:r + CHUNK, cols] = wu[r:r + CHUNK, cols] - gu[r:r + CHUNK, cols] * ka * bv[t:t + 1, :]
         copies.append(pltpu.make_async_copy(stage.at[r:r + CHUNK, :], wu_o.at[r:r + CHUNK, :], up_sems.at[i]))
         copies[-1].start()
     for copy in copies:
@@ -428,9 +449,10 @@
     outs = pl.pallas_call(
         main_kernel,
         out_shape=[pltpu.VMEM(SHAPES[UP], F32)] * 2 + [pltpu.VMEM(s, F32) for s in SHAPES[:2]]
-        + [pltpu.VMEM(s, F32) for s in stat_pairs] + [pltpu.VMEM((3, 8, LANES), F32)],
-        in_specs=[any_spec] * 8 + [vmem_spec] * 6 + [smem_spec] * 3,
-        out_specs=[vmem_spec] * 11,
+        + [pltpu.VMEM(s, F32) for s in stat_pairs]
+        + [pltpu.VMEM((3, 8, LANES), F32), pltpu.VMEM((512, LANES), F32), pltpu.VMEM(cols[UP], F32)],
+        in_specs=[any_spec] * 14 + [smem_spec] * 3,
+        out_specs=[vmem_spec] * 13,
         scratch_shapes=[
             pltpu.VMEM(SHAPES[DOWN], F32),
             pltpu.VMEM(SHAPES[GATE], F32),
@@ -441,31 +463,31 @@
             pltpu.VMEM((1408, LANES), F32),
             pltpu.VMEM((1408, LANES), F32),
             pltpu.VMEM((512, LANES), F32),
-            pltpu.VMEM((512, LANES), F32),
         ]
         + [pltpu.VMEM((8, n), F32) for m, n in SHAPES]
-        + [pltpu.VMEM(s, F32) for s in cols]
+        + [pltpu.VMEM(s, F32) for s in cols[:2]]
+        + [pltpu.VMEM(s, F32) for s in stat_pairs]
         + [pltpu.VMEM((COLS, *s), F32) for s in rows]
         + [pltpu.VMEM((ROWS, *s), F32) for s in cols]
         + [
             pltpu.VMEM((3, ROWS * COLS, 8, LANES), F32),
-            pltpu.VMEM((3, 8, LANES), F32),
-            pltpu.VMEM((3, 8, LANES), F32),
-            dma((7,)), dma((3, 5)), dma((3,)), dma((3,)), dma((3,)),
-            dma((3, 3)), dma((3, 3)), dma((3, 7)), dma((3, 7)),
+            pltpu.VMEM((3, 22, 8, LANES), F32),
+            pltpu.VMEM((3, 22, 8, LANES), F32),
+            dma((7,)), dma((3, 5)), dma((3,)), dma((6,)), dma((3,)), dma((3,)),
+            dma((4, 3)), dma((4, 3)), dma((3, 7)), dma((3, 7)),
         ],
         compiler_params=pltpu.CompilerParams(
             collective_id=0, has_side_effects=True, vmem_limit_bytes=VMEM_LIMIT),
         name="main",
     )(
         *[pltpu.with_memory_space_constraint(v, pltpu.HBM)
-          for v in (x_in, h_act, d_gate, d_up, d_out, w_gate, w_up, w_down)],
-        *stats, beta, rel, clip)
+          for v in (x_in, h_act, d_gate, d_up, d_out, w_gate, w_up, w_down, *stats)],
+        beta, rel, clip)
     held = [pltpu.with_memory_space_constraint(v, pltpu.VMEM) for v in outs]
     res = pl.pallas_call(
         update_kernel,
         out_shape=[jax.ShapeDtypeStruct(s, F32) for s in (SHAPES[UP], *SHAPES[:2], *stat_pairs)],
-        in_specs=[vmem_spec] * 11,
+        in_specs=[vmem_spec] * 13,
         out_specs=[any_spec] * 9,
         scratch_shapes=[pltpu.VMEM(SHAPES[UP], F32), dma((8,)), dma((8,))],
         compiler_params=pltpu.CompilerParams(vmem_limit_bytes=VMEM_LIMIT),

time: 47.7 us -> 43.5 us (0.912)
  Pallas kernels: 44.7 us -> 40.6 us
    pallas_call x1, Pallas kernels: 38.4 us -> 34.5 us  [local_program(): pl.pallas_call(main_kernel, out_shape=[pltpu.VMEM(SHAPES[UP], F32)] * 2 +...]
where the time goes in v3:
time: 43.5 us; the launch traced here: 43.4 us
  Pallas kernels  40.6 us (93%)
  between operations  2.75 us (6%)
    pallas_call x1, Pallas kernels, local_program(): pl.pallas_call(main_kernel, out_shape=[pltpu.VMEM(SHAPES[UP], F32)] * 2 +...  34.5 us
    pallas_call x1, Pallas kernels, local_program(): pl.pallas_call(update_kernel, out_shape=[jax.ShapeDtypeStruct(s, F32) for...  6.18 us

profile of v3, /device:TPU:0, one launch (start us, length us, event | category | flops | bytes accessed | tf_op | source)
XLA Modules:
  0.0 43.4 jit_solution(9001957315169323762)
XLA Ops:
  2.6 34.5 %main.1 = (f32[512,2816]{1,0:T(8,128)S(1)}, f32[512,2816]{1,0:T(8,128)S(1)}, f32[1408,1024]{1,0:T(8,128)S(1)}, f32[512,2816]{1,0:T(8,128)S(1)}, f32[11,128]{1,0:...) custom-call(bf16[2048,512]{1,0:T(8,128)(2,1)} %x_hbm.1, ...), custom_call_target="tpu_custom_call" | custom-call | tf_op jit(solution)/shard_map/main/pallas_call | solution.py:449
  37.1 6.2 %update.1 = (f32[512,2816]{1,0:T(8,128)}, f32[1408,1024]{1,0:T(8,128)}, f32[512,2816]{1,0:T(8,128)}, f32[11,128]{1,0:T(8,128)}, f32[8,128]{1,0:T(8,128)}, /*inde...) custom-call(f32[512,2816]{1,0:T(8,128)S(1)} %get-tuple-element.31.gu, ...), custom_call_target="tpu_custom_call" | custom-call | tf_op jit(solution)/shard_map/update/pallas_call | solution.py:487

commit v4 on v3

--- a/solution.py
+++ b/solution.py
@@ -54,20 +54,14 @@
         pl.semaphore_signal(barrier, inc=1, device_id=peer(dc, dr), device_id_type=MESH)
 
 
-def scalar_copies(buf, send, recv):
-    _, c, r = place()
-    me = c * ROWS + r
-    return [
-        pltpu.make_async_remote_copy(
-            src_ref=buf.at[me], dst_ref=buf.at[me], send_sem=send.at[i], recv_sem=recv.at[i],
-            device_id=peer(*OTHERS[i]), device_id_type=MESH)
-        for i in range(len(OTHERS))
-    ]
+def remote(ref, send, recv, to):
+    return pltpu.make_async_remote_copy(
+        src_ref=ref, dst_ref=ref, send_sem=send, recv_sem=recv, device_id=to, device_id_type=MESH)
 
 
 def scalar_tile(s, w, r):
     rows = [jnp.sum(v, axis=0, keepdims=True) for v in (s, w, r)]
-    return jnp.concatenate(rows + [jnp.zeros((5, LANES), F32)], axis=0)
+    return jnp.concatenate(rows + [jnp.zeros((1, LANES), F32)], axis=0)
 
 
 def step_of(mat, buf, rel, clip):
@@ -91,7 +85,7 @@
     gu, wu, wd, wg, rd_new, cd_new, rg_new, cg_new, ru_new, cu_new, kap, abc_u, bv_u,
     gd, gg, ring, xt, hs, ht, rowacc, abc_d, abc_g, cacc_d, cacc_g, cacc_u,
     bv_d, bv_g, rd, cd, rg, cg, ru, cu, rbuf_d, rbuf_g, rbuf_u, cbuf_d, cbuf_g, cbuf_u, sbuf, sacc, wacc,
-    ring_sem, h_sem, w_sem, old_sem, r_send, r_recv, c_send, c_recv, s_send, s_recv,
+    sem, r_send, r_recv, c_send, c_recv, s_send, s_recv,
 ):
     G, W = (gd, gg, gu), (wd, wg, wu)
     d_hbm, w_hbm = (do_hbm, dg_hbm, du_hbm), (wd_hbm, wg_hbm, wu_hbm)
@@ -104,11 +98,12 @@
     def piece_copies(p):
         ks = slice(*PIECES[p])
         return (
-            pltpu.make_async_copy(h_hbm.at[ks, :], hs.at[ks, :], h_sem.at[0, p]),
-            pltpu.make_async_copy(do_hbm.at[ks, :], ring.at[0, ks, :], h_sem.at[1, p]),
+            pltpu.make_async_copy(h_hbm.at[ks, :], hs.at[ks, :], sem.at[2 * p]),
+            pltpu.make_async_copy(do_hbm.at[ks, :512], ring.at[0, ks, :512], sem.at[2 * p + 1]),
         )
 
-    x_copy = pltpu.make_async_copy(x_hbm, ring.at[2, :, :512], h_sem.at[2, 0])
+    x_copy = pltpu.make_async_copy(x_hbm, ring.at[2, :, :512], sem.at[10])
+    right_copy = pltpu.make_async_copy(do_hbm.at[:, 512:], ring.at[0, :, 512:], sem.at[11])
 
     places = (
         ring.at[1], hs.at[:, :1024], ring.at[2, :, :768],
@@ -117,36 +112,42 @@
 
     def d_copy(j):
         mat, n0, n1 = BLOCKS[j]
-        return pltpu.make_async_copy(d_hbm[mat].at[:, n0:n1], places[j], ring_sem.at[j])
+        return pltpu.make_async_copy(d_hbm[mat].at[:, n0:n1], places[j], sem.at[(12, 13, 6, 7, 10, 8, 12)[j]])
 
     old_copies = [
-        pltpu.make_async_copy(src, dst, old_sem.at[i])
+        pltpu.make_async_copy(src, dst, sem.at[i])
         for i, (src, dst) in enumerate(zip((rd_hbm, cd_hbm, rg_hbm, cg_hbm, ru_hbm, cu_hbm), (rd, cd, rg, cg, ru, cu)))
     ]
 
     def w_copy(mat):
-        return pltpu.make_async_copy(w_hbm[mat], W[mat], w_sem.at[mat])
-
-    def col_copies(mat, part, sem):
-        return [
-            pltpu.make_async_remote_copy(
-                src_ref=cbuf[mat].at[me_r, part], dst_ref=cbuf[mat].at[me_r, part],
-                send_sem=c_send.at[sem, d - 1], recv_sem=c_recv.at[sem, d - 1],
-                device_id=peer(0, d), device_id_type=MESH)
-            for d in (1, 2, 3)
-        ]
-
-    early = col_copies(UP, slice(0, EARLY_COLS), 3)
-
-    def sum_copies(mat):
-        row = pltpu.make_async_remote_copy(
-            src_ref=rbuf[mat].at[me_c], dst_ref=rbuf[mat].at[me_c],
-            send_sem=r_send.at[mat], recv_sem=r_recv.at[mat],
-            device_id=peer(1, 0), device_id_type=MESH)
-        return [row, *col_copies(mat, slice(EARLY_COLS if mat == UP else 0, SHAPES[mat][1] // LANES), mat)]
-
-    def tiles(mat):
-        return scalar_copies(sbuf.at[mat], s_send.at[mat], s_recv.at[mat])
+        return pltpu.make_async_copy(w_hbm[mat], W[mat], sem.at[(9, 11, 13)[mat]])
+
+    late = slice(EARLY_COLS, SHAPES[UP][1] // LANES)
+    COL_GROUPS = ((DOWN, slice(0, 8), 0), (GATE, slice(0, 22), 0), (UP, late, 0), (UP, slice(0, EARLY_COLS), 1))
+    EARLY = 3
+
+    def start_row(mat):
+        row_copy(mat).start()
+
+    def row_copy(mat):
+        return remote(rbuf[mat].at[me_c], r_send.at[0], r_recv.at[mat], peer(1, 0))
+
+    def start_cols(group):
+        mat, part, send = COL_GROUPS[group]
+        for d in (1, 2, 3):
+            remote(cbuf[mat].at[me_r, part], c_send.at[send], c_recv.at[group], peer(0, d)).start()
+
+    def all_cols(group):
+        mat, part, send = COL_GROUPS[group]
+        return remote(cbuf[mat].at[0:3, part], c_send.at[send], c_recv.at[group], peer(0, 1))
+
+    def start_tiles(mat):
+        me = me_c * ROWS + me_r
+        for dc, dr in OTHERS:
+            remote(sbuf.at[mat, me], s_send.at[0], s_recv.at[mat], peer(dc, dr)).start()
+
+    def all_tiles(mat):
+        return remote(sbuf.at[mat, 0:7], s_send.at[0], s_recv.at[mat], peer(0, 1))
 
     def start(copies):
         for c in copies:
@@ -155,10 +156,6 @@
     def wait(copies):
         for c in copies:
             c.wait()
-
-    def wait_recv(copies):
-        for c in copies:
-            c.wait_recv()
 
     def stats_units(mat, n0, n1):
         units = []
@@ -297,12 +294,20 @@
         ks = slice(*PIECES[p])
         out = []
         for r in range(0, 1408, 352):
-            for c in range(0, 1024, 512):
-                def dot(r=r, c=c):
-                    rs, cs = slice(r, r + 352), slice(c, c + 512)
-                    part = jnp.dot(ht[rs, ks], ring[0, ks, cs], preferred_element_type=F32)
-                    gd[rs, cs] = part if p == 0 else gd[rs, cs] + part
-                out.append(dot)
+            def dot(r=r):
+                rs = slice(r, r + 352)
+                part = jnp.dot(ht[rs, ks], ring[0, ks, :512], preferred_element_type=F32)
+                gd[rs, :512] = part if p == 0 else gd[rs, :512] + part
+            out.append(dot)
+        return out
+
+    def right_dots():
+        out = []
+        for r in range(0, 1408, 352):
+            def dot(r=r):
+                rs = slice(r, r + 352)
+                gd[rs, 512:] = jnp.dot(ht[rs, :], ring[0, :, 512:], preferred_element_type=F32)
+            out.append(dot)
         return out
 
     def dots_of(j):
@@ -329,12 +334,12 @@
 
     for p in (0, 1, 2):
         start(piece_copies(p))
-    start(old_copies)
     barrier = pltpu.get_barrier_semaphore()
     signal_entry(barrier)
     wait(piece_copies(0))
     start(piece_copies(3))
     start(piece_copies(4))
+    right_copy.start()
     x_copy.start()
     run(h_units(0))
     for p in range(4):
@@ -343,86 +348,102 @@
             d_copy(0).start()
         interleave(down_dots(p), h_units(p + 1))
     d_copy(1).start()
+    interleave(down_dots(4), [])
+    start(old_copies)
+    right_copy.wait()
     x_copy.wait()
-    interleave(down_dots(4), x_units())
+    interleave(right_dots(), x_units() + stats_units(DOWN, 0, 512))
     d_copy(2).start()
-    w_copy(DOWN).start()
     d_copy(3).start()
     d_copy(5).start()
+    w_copy(DOWN).start()
 
     d_copy(0).wait()
     wait(old_copies)
-    interleave(dots_of(0), stats_units(DOWN, 0, 1024) + sums_units(DOWN))
+    interleave(dots_of(0), stats_units(DOWN, 512, 1024) + sums_units(DOWN))
     pl.semaphore_wait(barrier, len(OTHERS))
-    start(sum_copies(DOWN))
+    start_row(DOWN)
+    start_cols(DOWN)
     d_copy(4).start()
     w_copy(GATE).start()
 
     d_copy(1).wait()
     d_copy(2).wait()
-    w_copy(DOWN).wait()
-    interleave(dots_of(1), stats_units(GATE, 0, 1024) + w2_units(DOWN)[:11])
-    interleave(dots_of(2), w2_units(DOWN)[11:] + stats_units(GATE, 1024, 2048))
+    interleave(dots_of(1), stats_units(GATE, 0, 1024))
+    interleave(dots_of(2), stats_units(GATE, 1024, 2048))
     d_copy(6).start()
     w_copy(UP).start()
 
     d_copy(3).wait()
     interleave(dots_of(3), stats_units(GATE, 2048, 2816) + sums_units(GATE))
-    start(sum_copies(GATE))
+    row_copy(DOWN).wait_send()
+    all_cols(DOWN).wait_send()
+    start_row(GATE)
+    start_cols(GATE)
 
     d_copy(4).wait()
     d_copy(5).wait()
-    w_copy(GATE).wait()
-    wait_recv(sum_copies(DOWN))
-    interleave(dots_of(4), factor_units(DOWN) + scale_units(DOWN) + stats_units(UP, 0, 512))
-    interleave(dots_of(5), tile_unit(DOWN) + w2_units(GATE) + stats_units(UP, 512, 1536))
-    start(tiles(DOWN))
+    row_copy(DOWN).wait_recv()
+    all_cols(DOWN).wait_recv()
+    interleave(dots_of(4), factor_units(DOWN) + scale_units(DOWN))
+    interleave(dots_of(5), stats_units(UP, 0, 512) + stats_units(UP, 512, 1536))
 
     d_copy(6).wait()
-    wait_recv(sum_copies(GATE))
+    w_copy(DOWN).wait()
     interleave(
         dots_of(6),
-        factor_units(GATE) + scale_units(GATE) + tile_unit(GATE) + stats_units(UP, 1536, 2048)
-        + col_units(UP, 0, EARLY_COLS))
-    start(tiles(GATE))
-    start(early)
+        w2_units(DOWN) + tile_unit(DOWN) + stats_units(UP, 1536, 2048) + col_units(UP, 0, EARLY_COLS))
+    start_cols(EARLY)
+    start_tiles(DOWN)
 
     run(stats_units(UP, 2048, 2816) + row_units(UP) + col_units(UP, EARLY_COLS, 22))
-    start(sum_copies(UP))
+    row_copy(GATE).wait_send()
+    all_cols(GATE).wait_send()
+    start_row(UP)
+    start_cols(UP)
+    w_copy(GATE).wait()
     w_copy(UP).wait()
+    row_copy(GATE).wait_recv()
+    all_cols(GATE).wait_recv()
+    run(factor_units(GATE) + scale_units(GATE) + w2_units(GATE) + tile_unit(GATE))
+    all_tiles(DOWN).wait_send()
+    start_tiles(GATE)
     run(w2_units(UP))
-    wait_recv(tiles(DOWN))
+    all_cols(EARLY).wait_recv()
+    row_copy(UP).wait_recv()
+    all_cols(UP).wait_recv()
+    run(factor_units(UP) + scale_units(UP) + tile_unit(UP))
+    all_tiles(GATE).wait_send()
+    start_tiles(UP)
+    all_tiles(DOWN).wait_recv()
     run(update_units(DOWN))
-    wait_recv(early)
-    wait_recv(sum_copies(UP))
-    run(factor_units(UP) + scale_units(UP) + tile_unit(UP))
-    start(tiles(UP))
-    wait_recv(tiles(GATE))
+    all_tiles(GATE).wait_recv()
     run(update_units(GATE))
-    for copies in [sum_copies(mat) for mat in range(3)] + [early, tiles(DOWN), tiles(GATE), tiles(UP)]:
-        for c in copies:
-            c.wait_send()
-    wait_recv(tiles(UP))
+    row_copy(UP).wait_send()
+    all_cols(UP).wait_send()
+    all_cols(EARLY).wait_send()
+    all_tiles(UP).wait_send()
+    all_tiles(UP).wait_recv()
     kap[UP] = step_of(UP, sbuf.at[UP], rel[0], clip[0])
 
 
 def update_kernel(
     gu, wu, wd, wg, rd, cd, rg, cg, ru, cu, kap, abc, bv,
-    wu_o, wd_o, wg_o, rd_o, cd_o, rg_o, cg_o, ru_o, cu_o, stage, sems, up_sems,
+    wu_o, wd_o, wg_o, rd_o, cd_o, rg_o, cg_o, ru_o, cu_o, stage, sem,
 ):
     srcs = (wd, wg, rd, cd, rg, cg, ru, cu)
     dsts = (wd_o, wg_o, rd_o, cd_o, rg_o, cg_o, ru_o, cu_o)
-    copies = [pltpu.make_async_copy(src, dst, sems.at[i]) for i, (src, dst) in enumerate(zip(srcs, dsts))]
+    copies = [pltpu.make_async_copy(src, dst, sem) for src, dst in zip(srcs, dsts)]
     for c in copies:
         c.start()
     m, n = SHAPES[UP]
     k = kap[UP, 0:1, :]
-    for i, r in enumerate(range(0, m, CHUNK)):
+    for r in range(0, m, CHUNK):
         ka = abc[r:r + CHUNK, :] * k
         for t in range(n // LANES):
             cols = slice(t * LANES, (t + 1) * LANES)
             stage[r:r + CHUNK, cols] = wu[r:r + CHUNK, cols] - gu[r:r + CHUNK, cols] * ka * bv[t:t + 1, :]
-        copies.append(pltpu.make_async_copy(stage.at[r:r + CHUNK, :], wu_o.at[r:r + CHUNK, :], up_sems.at[i]))
+        copies.append(pltpu.make_async_copy(stage.at[r:r + CHUNK, :], wu_o.at[r:r + CHUNK, :], sem))
         copies[-1].start()
     for copy in copies:
         copy.wait()
@@ -470,11 +491,10 @@
         + [pltpu.VMEM((COLS, *s), F32) for s in rows]
         + [pltpu.VMEM((ROWS, *s), F32) for s in cols]
         + [
-            pltpu.VMEM((3, ROWS * COLS, 8, LANES), F32),
+            pltpu.VMEM((3, ROWS * COLS, 4, LANES), F32),
             pltpu.VMEM((3, 22, 8, LANES), F32),
             pltpu.VMEM((3, 22, 8, LANES), F32),
-            dma((7,)), dma((3, 5)), dma((3,)), dma((6,)), dma((3,)), dma((3,)),
-            dma((4, 3)), dma((4, 3)), dma((3, 7)), dma((3, 7)),
+            dma((14,)), dma((1,)), dma((3,)), dma((2,)), dma((4,)), dma((1,)), dma((3,)),
         ],
         compiler_params=pltpu.CompilerParams(
             collective_id=0, has_side_effects=True, vmem_limit_bytes=VMEM_LIMIT),
@@ -489,7 +509,7 @@
         out_shape=[jax.ShapeDtypeStruct(s, F32) for s in (SHAPES[UP], *SHAPES[:2], *stat_pairs)],
         in_specs=[vmem_spec] * 13,
         out_specs=[any_spec] * 9,
-        scratch_shapes=[pltpu.VMEM(SHAPES[UP], F32), dma((8,)), dma((8,))],
+        scratch_shapes=[pltpu.VMEM(SHAPES[UP], F32), dma],
         compiler_params=pltpu.CompilerParams(vmem_limit_bytes=VMEM_LIMIT),
         name="update",
     )(*held)

time: 43.5 us -> 41 us (0.943)
  Pallas kernels: 40.6 us -> 38.1 us
    pallas_call x1, Pallas kernels: 34.5 us -> 32.1 us  [local_program(): pl.pallas_call(main_kernel, out_shape=[pltpu.VMEM(SHAPES[UP], F32)] * 2 +...]
where the time goes in v4:
time: 41 us; the launch traced here: 40.9 us
  Pallas kernels  38.1 us (93%)
  between operations  2.75 us (7%)
    pallas_call x1, Pallas kernels, local_program(): pl.pallas_call(main_kernel, out_shape=[pltpu.VMEM(SHAPES[UP], F32)] * 2 +...  32.1 us
    pallas_call x1, Pallas kernels, local_program(): pl.pallas_call(update_kernel, out_shape=[jax.ShapeDtypeStruct(s, F32) for...  6.05 us

profile of v4, /device:TPU:0, one launch (start us, length us, event | category | flops | bytes accessed | tf_op | source)
XLA Modules:
  0.0 40.9 jit_solution(10433250264441248754)
XLA Ops:
  2.6 32.1 %main.1 = (f32[512,2816]{1,0:T(8,128)S(1)}, f32[512,2816]{1,0:T(8,128)S(1)}, f32[1408,1024]{1,0:T(8,128)S(1)}, f32[512,2816]{1,0:T(8,128)S(1)}, f32[11,128]{1,0:...) custom-call(bf16[2048,512]{1,0:T(8,128)(2,1)} %x_hbm.1, ...), custom_call_target="tpu_custom_call" | custom-call | tf_op jit(solution)/shard_map/main/pallas_call | solution.py:470
  34.7 6.0 %update.1 = (f32[512,2816]{1,0:T(8,128)}, f32[1408,1024]{1,0:T(8,128)}, f32[512,2816]{1,0:T(8,128)}, f32[11,128]{1,0:T(8,128)}, f32[8,128]{1,0:T(8,128)}, /*inde...) custom-call(f32[512,2816]{1,0:T(8,128)S(1)} %get-tuple-element.31.gu, ...), custom_call_target="tpu_custom_call" | custom-call | tf_op jit(solution)/shard_map/update/pallas_call | solution.py:507

commit v5 on v4

--- a/solution.py
+++ b/solution.py
@@ -64,27 +64,30 @@
     return jnp.concatenate(rows + [jnp.zeros((1, LANES), F32)], axis=0)
 
 
-def step_of(mat, buf, rel, clip):
-    mt, nt = TOTALS[mat]
+def sums_of(buf):
     tot = buf[0]
     for i in range(1, ROWS * COLS):
         tot = tot + buf[i]
-    tot = jnp.sum(tot, axis=1, keepdims=True)
+    return jnp.broadcast_to(jnp.sum(tot, axis=1, keepdims=True), tot.shape)
+
+
+def step_of(mat, tot, rel, clip):
+    mt, nt = TOTALS[mat]
     s, w, r = tot[0:1, :], tot[1:2, :], tot[2:3, :]
     r_mean = r * (1.0 / (COLS * mt))
     u_rms = jnp.sqrt(s * (1.0 / (mt * nt)) * r_mean)
     w_rms = jnp.sqrt(w * (1.0 / (mt * nt)))
     step = rel * jnp.maximum(EPS_SCALE, w_rms)
-    k = step * jnp.sqrt(r_mean) / jnp.maximum(1.0, u_rms / clip)
-    return jnp.broadcast_to(k, (8, LANES))
+    return step * jnp.sqrt(r_mean) / jnp.maximum(1.0, u_rms / clip)
 
 
 def main_kernel(
     x_hbm, h_hbm, dg_hbm, du_hbm, do_hbm, wg_hbm, wu_hbm, wd_hbm,
-    rg_hbm, cg_hbm, ru_hbm, cu_hbm, rd_hbm, cd_hbm, beta, rel, clip,
-    gu, wu, wd, wg, rd_new, cd_new, rg_new, cg_new, ru_new, cu_new, kap, abc_u, bv_u,
-    gd, gg, ring, xt, hs, ht, rowacc, abc_d, abc_g, cacc_d, cacc_g, cacc_u,
-    bv_d, bv_g, rd, cd, rg, cg, ru, cu, rbuf_d, rbuf_g, rbuf_u, cbuf_d, cbuf_g, cbuf_u, sbuf, sacc, wacc,
+    rg_hbm, cg_hbm, ru_hbm, cu_hbm, rd_hbm, cd_hbm, beta,
+    gd, gg, gu, wd, wg, wu, rd_new, cd_new, rg_new, cg_new, ru_new, cu_new, sums,
+    abc_d, abc_g, abc_u, bv_d, bv_g, bv_u,
+    ring, xt, hs, ht, rowacc, cacc_d, cacc_g, cacc_u,
+    rd, cd, rg, cg, ru, cu, rbuf_d, rbuf_g, rbuf_u, cbuf_d, cbuf_g, cbuf_u, sbuf, sacc, wacc,
     sem, r_send, r_recv, c_send, c_recv, s_send, s_recv,
 ):
     G, W = (gd, gg, gu), (wd, wg, wu)
@@ -238,28 +241,11 @@
             def unit(i=i):
                 acc = None
                 rows = slice(i * CHUNK, (i + 1) * CHUNK)
+                for t in range(n // LANES):
+                    h = G[mat][rows, t * LANES:(t + 1) * LANES] * bv[mat][t:t + 1, :]
+                    acc = h * h if acc is None else acc + h * h
                 a = abc[mat][rows, :]
-                for t in range(n // LANES):
-                    h = G[mat][rows, t * LANES:(t + 1) * LANES] * a * bv[mat][t:t + 1, :]
-                    f = fold(h * h)
-                    acc = f if acc is None else acc + f
-                sacc[mat, i] = acc
-            units.append(unit)
-        return units
-
-    def update_units(mat):
-        def step():
-            kap[mat] = step_of(mat, sbuf.at[mat], rel[0], clip[0])
-
-        units = [step]
-        m, n = SHAPES[mat]
-        for r in range(0, m, CHUNK):
-            def unit(r=r):
-                ka = abc[mat][r:r + CHUNK, :] * kap[mat, 0:1, :]
-                for t in range(n // LANES):
-                    cols = slice(t * LANES, (t + 1) * LANES)
-                    W[mat][r:r + CHUNK, cols] = (
-                        W[mat][r:r + CHUNK, cols] - G[mat][r:r + CHUNK, cols] * ka * bv[mat][t:t + 1, :])
+                sacc[mat, i] = fold(acc * (a * a))
             units.append(unit)
         return units
 
@@ -416,40 +402,47 @@
     all_tiles(GATE).wait_send()
     start_tiles(UP)
     all_tiles(DOWN).wait_recv()
-    run(update_units(DOWN))
+    sums[DOWN] = sums_of(sbuf.at[DOWN])
     all_tiles(GATE).wait_recv()
-    run(update_units(GATE))
+    sums[GATE] = sums_of(sbuf.at[GATE])
     row_copy(UP).wait_send()
     all_cols(UP).wait_send()
     all_cols(EARLY).wait_send()
     all_tiles(UP).wait_send()
     all_tiles(UP).wait_recv()
-    kap[UP] = step_of(UP, sbuf.at[UP], rel[0], clip[0])
+    sums[UP] = sums_of(sbuf.at[UP])
 
 
 def update_kernel(
-    gu, wu, wd, wg, rd, cd, rg, cg, ru, cu, kap, abc, bv,
-    wu_o, wd_o, wg_o, rd_o, cd_o, rg_o, cg_o, ru_o, cu_o, stage, sem,
+    gd, gg, gu, wd, wg, wu, rd, cd, rg, cg, ru, cu, sums, abc_d, abc_g, abc_u, bv_d, bv_g, bv_u, rel, clip,
+    wd_o, wg_o, wu_o, rd_o, cd_o, rg_o, cg_o, ru_o, cu_o, stage_d, stage_g, stage_u, sem,
 ):
-    srcs = (wd, wg, rd, cd, rg, cg, ru, cu)
-    dsts = (wd_o, wg_o, rd_o, cd_o, rg_o, cg_o, ru_o, cu_o)
-    copies = [pltpu.make_async_copy(src, dst, sem) for src, dst in zip(srcs, dsts)]
-    for c in copies:
-        c.start()
-    m, n = SHAPES[UP]
-    k = kap[UP, 0:1, :]
-    for r in range(0, m, CHUNK):
-        ka = abc[r:r + CHUNK, :] * k
-        for t in range(n // LANES):
-            cols = slice(t * LANES, (t + 1) * LANES)
-            stage[r:r + CHUNK, cols] = wu[r:r + CHUNK, cols] - gu[r:r + CHUNK, cols] * ka * bv[t:t + 1, :]
-        copies.append(pltpu.make_async_copy(stage.at[r:r + CHUNK, :], wu_o.at[r:r + CHUNK, :], sem))
+    copies = []
+
+    def write(src, dst):
+        copies.append(pltpu.make_async_copy(src, dst, sem))
         copies[-1].start()
+
+    steps = [step_of(mat, sums[mat], rel[...], clip[...]) for mat in range(3)]
+    for mat, (g, w, abc, bv, stage, out) in enumerate((
+        (gd, wd, abc_d, bv_d, stage_d, wd_o), (gg, wg, abc_g, bv_g, stage_g, wg_o), (gu, wu, abc_u, bv_u, stage_u, wu_o),
+    )):
+        m, n = SHAPES[mat]
+        for r in range(0, m, CHUNK):
+            rows = slice(r, r + CHUNK)
+            ka = abc[rows, :] * steps[mat]
+            for t in range(n // LANES):
+                cols = slice(t * LANES, (t + 1) * LANES)
+                stage[rows, cols] = w[rows, cols] - g[rows, cols] * ka * bv[t:t + 1, :]
+            write(stage.at[rows, :], out.at[rows, :])
+        if mat == DOWN:
+            for src, dst in ((rd, rd_o), (cd, cd_o), (rg, rg_o), (cg, cg_o), (ru, ru_o), (cu, cu_o)):
+                write(src, dst)
     for copy in copies:
         copy.wait()
 
 
-VMEM_LIMIT = 41 * 1024 * 1024
+VMEM_LIMIT = 30880000
 
 
 def local_program(x_in, h_act, d_gate, d_up, d_out, w_gate, w_up, w_down, r_gate, c_gate, r_up, c_up, r_down, c_down, beta_two, rel_step, clip_thr):
@@ -461,7 +454,8 @@
         return (v // LANES, LANES)
 
     stats = [v.reshape(stat_shape(v.shape[0])) for v in (r_gate, c_gate, r_up, c_up, r_down, c_down)]
-    beta, rel, clip = [v.reshape(1) for v in (beta_two, rel_step, clip_thr)]
+    beta = beta_two.reshape(1)
+    rel, clip = [lax.ppermute(v.reshape(1, 1), "data", [(0, 1), (1, 0)]) for v in (rel_step, clip_thr)]
     rows = [stat_shape(m) for m, n in SHAPES]
     cols = [stat_shape(n) for m, n in SHAPES]
     dma = pltpu.SemaphoreType.DMA
@@ -469,24 +463,18 @@
     stat_pairs = [s for pair in zip(rows, cols) for s in pair]
     outs = pl.pallas_call(
         main_kernel,
-        out_shape=[pltpu.VMEM(SHAPES[UP], F32)] * 2 + [pltpu.VMEM(s, F32) for s in SHAPES[:2]]
-        + [pltpu.VMEM(s, F32) for s in stat_pairs]
-        + [pltpu.VMEM((3, 8, LANES), F32), pltpu.VMEM((512, LANES), F32), pltpu.VMEM(cols[UP], F32)],
-        in_specs=[any_spec] * 14 + [smem_spec] * 3,
-        out_specs=[vmem_spec] * 13,
+        out_shape=[pltpu.VMEM(s, F32) for s in (*SHAPES, *SHAPES, *stat_pairs, (3, 4, LANES))]
+        + [pltpu.VMEM((m, LANES), F32) for m, n in SHAPES] + [pltpu.VMEM(s, F32) for s in cols],
+        in_specs=[any_spec] * 14 + [smem_spec],
+        out_specs=[vmem_spec] * 19,
         scratch_shapes=[
-            pltpu.VMEM(SHAPES[DOWN], F32),
-            pltpu.VMEM(SHAPES[GATE], F32),
             pltpu.VMEM((3, K, 1024), BF16),
             pltpu.VMEM((512, K), BF16),
             pltpu.VMEM((K, 1408), BF16),
             pltpu.VMEM((1408, K), BF16),
             pltpu.VMEM((1408, LANES), F32),
-            pltpu.VMEM((1408, LANES), F32),
-            pltpu.VMEM((512, LANES), F32),
         ]
         + [pltpu.VMEM((8, n), F32) for m, n in SHAPES]
-        + [pltpu.VMEM(s, F32) for s in cols[:2]]
         + [pltpu.VMEM(s, F32) for s in stat_pairs]
         + [pltpu.VMEM((COLS, *s), F32) for s in rows]
         + [pltpu.VMEM((ROWS, *s), F32) for s in cols]
@@ -502,18 +490,18 @@
     )(
         *[pltpu.with_memory_space_constraint(v, pltpu.HBM)
           for v in (x_in, h_act, d_gate, d_up, d_out, w_gate, w_up, w_down, *stats)],
-        beta, rel, clip)
-    held = [pltpu.with_memory_space_constraint(v, pltpu.VMEM) for v in outs]
+        beta)
+    held = [pltpu.with_memory_space_constraint(v, pltpu.VMEM) for v in (*outs, rel, clip)]
     res = pl.pallas_call(
         update_kernel,
-        out_shape=[jax.ShapeDtypeStruct(s, F32) for s in (SHAPES[UP], *SHAPES[:2], *stat_pairs)],
-        in_specs=[vmem_spec] * 13,
+        out_shape=[jax.ShapeDtypeStruct(s, F32) for s in (*SHAPES, *stat_pairs)],
+        in_specs=[vmem_spec] * 21,
         out_specs=[any_spec] * 9,
-        scratch_shapes=[pltpu.VMEM(SHAPES[UP], F32), dma],
+        scratch_shapes=[pltpu.VMEM(s, F32) for s in SHAPES] + [dma],
         compiler_params=pltpu.CompilerParams(vmem_limit_bytes=VMEM_LIMIT),
         name="update",
     )(*held)
-    up, down, gate, rd_n, cd_n, rg_n, cg_n, ru_n, cu_n = res
+    down, gate, up, rd_n, cd_n, rg_n, cg_n, ru_n, cu_n = res
     flat = [v.reshape(-1) for v in (rg_n, cg_n, ru_n, cu_n, rd_n, cd_n)]
     return (gate, up, down, *flat)
 

time: 41 us -> 43 us (1.049)
  starting transfers between devices: 0 us -> 3.4 us
  between operations: 2.75 us -> 1.48 us
    ppermute x0 -> x2, starting transfers between devices: none -> 3.4 us  [local_program(): lax.ppermute(v.reshape(1, 1), 'data', [(0, 1), (1, 0)])]
    pallas_call x1, Pallas kernels: 32.1 us -> 30.7 us  [local_program(): pl.pallas_call(main_kernel, out_shape=[pltpu.VMEM(s, F32) for s in (*SHAP...]
    pallas_call x1, Pallas kernels: 6.05 us -> 7.33 us  [local_program(): pl.pallas_call(update_kernel, out_shape=[jax.ShapeDtypeStruct(s, F32) for...]
  transfers between devices with their start and end apart: 0 -> 2, of which waited for: 0 -> 0; matrix products, arithmetic and copies ran while one was open for 0% -> 0% of each run, Pallas kernels for 0% -> 71%
where the time goes in v5:
time: 43 us; the launch traced here: 42.9 us
  Pallas kernels  38 us (88%)
  starting transfers between devices  3.4 us (8%)
  between operations  1.48 us (3%)
    pallas_call x1, Pallas kernels, local_program(): pl.pallas_call(main_kernel, out_shape=[pltpu.VMEM(s, F32) for s in (*SHAP...  30.7 us
    pallas_call x1, Pallas kernels, local_program(): pl.pallas_call(update_kernel, out_shape=[jax.ShapeDtypeStruct(s, F32) for...  7.33 us
    ppermute x2, starting transfers between devices, local_program(): lax.ppermute(v.reshape(1, 1), 'data', [(0, 1), (1, 0)])  3.4 us
  transfers between devices with their start and end apart: 2, of which 0 were waited for; matrix products, arithmetic and copies ran while one was open for 0% of the time, Pallas kernels for 71%

profile of v5, /device:TPU:0, one launch (start us, length us, event | category | flops | bytes accessed | tf_op | source)
XLA Modules:
  0.0 42.9 jit_solution(6568009315346557864)
XLA Ops:
  0.6 3.3 %collective-permute-start = (f32[1,1]{1,0:T(1,128)}, f32[1,1]{1,0:T(1,128)}, u32[]{:S(2)}, u32[]{:S(2)}) collective-permute-start(f32[1,1]{1,0:T(1,128)} %bitcast.7), channel_id=1, source_target_pairs={{0,8},{8,0},{1,9},{9,1},{2,10},{10,2},{3,11},{11,3},{4,12},{12,4},... | collective-permute-start | bytes 20 | tf_op jit(solution)/shard_map/ppermute | solution.py:458
  4.0 0.1 collective-permute-start.1
  4.7 30.7 %main.1 = (f32[1408,1024]{1,0:T(8,128)S(1)}, f32[512,2816]{1,0:T(8,128)S(1)}, f32[512,2816]{1,0:T(8,128)S(1)}, f32[1408,1024]{1,0:T(8,128)S(1)}, f32[512,2816]{1...) custom-call(bf16[2048,512]{1,0:T(8,128)(2,1)} %x_hbm.1, ...), custom_call_target="tpu_custom_call" | custom-call | tf_op jit(solution)/shard_map/main/pallas_call | solution.py:464
  35.4 0.0 collective-permute-done.rel
  35.4 0.0 collective-permute-done.1.clip
  35.4 7.3 %update.1 = (f32[1408,1024]{1,0:T(8,128)}, f32[512,2816]{1,0:T(8,128)}, f32[512,2816]{1,0:T(8,128)}, f32[11,128]{1,0:T(8,128)}, f32[8,128]{1,0:T(8,128)}, /*inde...) custom-call(f32[1408,1024]{1,0:T(8,128)S(1)} %get-tuple-element.37.gd, ...), custom_call_target="tpu_custom_call" | custom-call | tf_op jit(solution)/shard_map/update/pallas_call | solution.py:495
Async XLA Ops:
  0.6 34.7 %collective-permute-start = (f32[1,1]{1,0:T(1,128)}, f32[1,1]{1,0:T(1,128)}, u32[]{:S(2)}, u32[]{:S(2)}) collective-permute-start(f32[1,1]{1,0:T(1,128)} %bitcast.7), channel_id=1, source_target_pairs={{0,8},{8,0},{1,9},{9,1},{2,10},{10,2},{3,11},{11,3},{4,12},{12,4},... | collective-permute-start | bytes 20 | tf_op jit(solution)/shard_map/ppermute | solution.py:458
  4.0 31.4 %collective-permute-start.1 = (f32[1,1]{1,0:T(1,128)}, f32[1,1]{1,0:T(1,128)}, u32[]{:S(2)}, u32[]{:S(2)}) collective-permute-start(f32[1,1]{1,0:T(1,128)} %bitcast.8), channel_id=1, source_target_pairs={{0,8},{8,0},{1,9},{9,1},{2,10},{10,2},{3,11},{11,3},{4,12},{12,4},... | collective-permute-start | bytes 20 | tf_op jit(solution)/shard_map/ppermute | solution.py:458

commit v6 on v4

--- a/solution.py
+++ b/solution.py
@@ -238,12 +238,11 @@
             def unit(i=i):
                 acc = None
                 rows = slice(i * CHUNK, (i + 1) * CHUNK)
+                for t in range(n // LANES):
+                    h = G[mat][rows, t * LANES:(t + 1) * LANES] * bv[mat][t:t + 1, :]
+                    acc = h * h if acc is None else acc + h * h
                 a = abc[mat][rows, :]
-                for t in range(n // LANES):
-                    h = G[mat][rows, t * LANES:(t + 1) * LANES] * a * bv[mat][t:t + 1, :]
-                    f = fold(h * h)
-                    acc = f if acc is None else acc + f
-                sacc[mat, i] = acc
+                sacc[mat, i] = fold(acc * (a * a))
             units.append(unit)
         return units
 
@@ -385,24 +384,22 @@
     d_copy(5).wait()
     row_copy(DOWN).wait_recv()
     all_cols(DOWN).wait_recv()
-    interleave(dots_of(4), factor_units(DOWN) + scale_units(DOWN))
-    interleave(dots_of(5), stats_units(UP, 0, 512) + stats_units(UP, 512, 1536))
+    interleave(dots_of(4) + dots_of(5), stats_units(UP, 0, 512) + factor_units(DOWN) + scale_units(DOWN))
 
     d_copy(6).wait()
-    w_copy(DOWN).wait()
-    interleave(
-        dots_of(6),
-        w2_units(DOWN) + tile_unit(DOWN) + stats_units(UP, 1536, 2048) + col_units(UP, 0, EARLY_COLS))
+    interleave(dots_of(6), stats_units(UP, 512, 1536) + stats_units(UP, 1536, 2048) + col_units(UP, 0, EARLY_COLS))
     start_cols(EARLY)
-    start_tiles(DOWN)
 
     run(stats_units(UP, 2048, 2816) + row_units(UP) + col_units(UP, EARLY_COLS, 22))
     row_copy(GATE).wait_send()
     all_cols(GATE).wait_send()
     start_row(UP)
     start_cols(UP)
+    w_copy(DOWN).wait()
     w_copy(GATE).wait()
     w_copy(UP).wait()
+    run(w2_units(DOWN) + tile_unit(DOWN))
+    start_tiles(DOWN)
     row_copy(GATE).wait_recv()
     all_cols(GATE).wait_recv()
     run(factor_units(GATE) + scale_units(GATE) + w2_units(GATE) + tile_unit(GATE))

time: 41 us -> 41 us (level)
  no operation moved by 1% of the time
where the time goes in v6:
time: 41 us; the launch traced here: 40.8 us
  Pallas kernels  38.1 us (93%)
  between operations  2.75 us (7%)
    pallas_call x1, Pallas kernels, local_program(): pl.pallas_call(main_kernel, out_shape=[pltpu.VMEM(SHAPES[UP], F32)] * 2 +...  32 us
    pallas_call x1, Pallas kernels, local_program(): pl.pallas_call(update_kernel, out_shape=[jax.ShapeDtypeStruct(s, F32) for...  6.05 us

profile of v6, /device:TPU:0, one launch (start us, length us, event | category | flops | bytes accessed | tf_op | source)
XLA Modules:
  0.0 40.8 jit_solution(17425367576787315477)
XLA Ops:
  2.6 32.0 %main.1 = (f32[512,2816]{1,0:T(8,128)S(1)}, f32[512,2816]{1,0:T(8,128)S(1)}, f32[1408,1024]{1,0:T(8,128)S(1)}, f32[512,2816]{1,0:T(8,128)S(1)}, f32[11,128]{1,0:...) custom-call(bf16[2048,512]{1,0:T(8,128)(2,1)} %x_hbm.1, ...), custom_call_target="tpu_custom_call" | custom-call | tf_op jit(solution)/shard_map/main/pallas_call | solution.py:467
  34.6 6.0 %update.1 = (f32[512,2816]{1,0:T(8,128)}, f32[1408,1024]{1,0:T(8,128)}, f32[512,2816]{1,0:T(8,128)}, f32[11,128]{1,0:T(8,128)}, f32[8,128]{1,0:T(8,128)}, /*inde...) custom-call(f32[512,2816]{1,0:T(8,128)S(1)} %get-tuple-element.31.gu, ...), custom_call_target="tpu_custom_call" | custom-call | tf_op jit(solution)/shard_map/update/pallas_call | solution.py:504

commit v7 on v6

--- a/solution.py
+++ b/solution.py
@@ -374,7 +374,8 @@
     w_copy(UP).start()
 
     d_copy(3).wait()
-    interleave(dots_of(3), stats_units(GATE, 2048, 2816) + sums_units(GATE))
+    w_copy(DOWN).wait()
+    interleave(dots_of(3), stats_units(GATE, 2048, 2816) + sums_units(GATE) + w2_units(DOWN)[:11])
     row_copy(DOWN).wait_send()
     all_cols(DOWN).wait_send()
     start_row(GATE)
@@ -384,22 +385,22 @@
     d_copy(5).wait()
     row_copy(DOWN).wait_recv()
     all_cols(DOWN).wait_recv()
-    interleave(dots_of(4) + dots_of(5), stats_units(UP, 0, 512) + factor_units(DOWN) + scale_units(DOWN))
+    interleave(dots_of(4) + dots_of(5), stats_units(UP, 0, 512) + factor_units(DOWN) + scale_units(DOWN) + w2_units(DOWN)[11:])
 
     d_copy(6).wait()
-    interleave(dots_of(6), stats_units(UP, 512, 1536) + stats_units(UP, 1536, 2048) + col_units(UP, 0, EARLY_COLS))
+    interleave(
+        dots_of(6),
+        tile_unit(DOWN) + stats_units(UP, 512, 1536) + stats_units(UP, 1536, 2048) + col_units(UP, 0, EARLY_COLS))
     start_cols(EARLY)
+    start_tiles(DOWN)
 
     run(stats_units(UP, 2048, 2816) + row_units(UP) + col_units(UP, EARLY_COLS, 22))
     row_copy(GATE).wait_send()
     all_cols(GATE).wait_send()
     start_row(UP)
     start_cols(UP)
-    w_copy(DOWN).wait()
     w_copy(GATE).wait()
     w_copy(UP).wait()
-    run(w2_units(DOWN) + tile_unit(DOWN))
-    start_tiles(DOWN)
     row_copy(GATE).wait_recv()
     all_cols(GATE).wait_recv()
     run(factor_units(GATE) + scale_units(GATE) + w2_units(GATE) + tile_unit(GATE))

time: 41 us -> 41 us (level)
  no operation moved by 1% of the time
where the time goes in v7:
time: 41 us; the launch traced here: 40.9 us
  Pallas kernels  38.1 us (93%)
  between operations  2.75 us (7%)
    pallas_call x1, Pallas kernels, local_program(): pl.pallas_call(main_kernel, out_shape=[pltpu.VMEM(SHAPES[UP], F32)] * 2 +...  32.1 us
    pallas_call x1, Pallas kernels, local_program(): pl.pallas_call(update_kernel, out_shape=[jax.ShapeDtypeStruct(s, F32) for...  6.05 us

profile of v7, /device:TPU:0, one launch (start us, length us, event | category | flops | bytes accessed | tf_op | source)
XLA Modules:
  0.0 40.9 jit_solution(8107394306879659466)
XLA Ops:
  2.6 32.1 %main.1 = (f32[512,2816]{1,0:T(8,128)S(1)}, f32[512,2816]{1,0:T(8,128)S(1)}, f32[1408,1024]{1,0:T(8,128)S(1)}, f32[512,2816]{1,0:T(8,128)S(1)}, f32[11,128]{1,0:...) custom-call(bf16[2048,512]{1,0:T(8,128)(2,1)} %x_hbm.1, ...), custom_call_target="tpu_custom_call" | custom-call | tf_op jit(solution)/shard_map/main/pallas_call | solution.py:468
  34.7 6.0 %update.1 = (f32[512,2816]{1,0:T(8,128)}, f32[1408,1024]{1,0:T(8,128)}, f32[512,2816]{1,0:T(8,128)}, f32[11,128]{1,0:T(8,128)}, f32[8,128]{1,0:T(8,128)}, /*inde...) custom-call(f32[512,2816]{1,0:T(8,128)S(1)} %get-tuple-element.31.gu, ...), custom_call_target="tpu_custom_call" | custom-call | tf_op jit(solution)/shard_map/update/pallas_call | solution.py:505

commit v8 on v6

--- a/solution.py
+++ b/solution.py
@@ -83,8 +83,9 @@
     x_hbm, h_hbm, dg_hbm, du_hbm, do_hbm, wg_hbm, wu_hbm, wd_hbm,
     rg_hbm, cg_hbm, ru_hbm, cu_hbm, rd_hbm, cd_hbm, beta, rel, clip,
     gu, wu, wd, wg, rd_new, cd_new, rg_new, cg_new, ru_new, cu_new, kap, abc_u, bv_u,
-    gd, gg, ring, xt, hs, ht, rowacc, abc_d, abc_g, cacc_d, cacc_g, cacc_u,
-    bv_d, bv_g, rd, cd, rg, cg, ru, cu, rbuf_d, rbuf_g, rbuf_u, cbuf_d, cbuf_g, cbuf_u, sbuf, sacc, wacc,
+    gg, abc_g, bv_g,
+    gd, ring, xt, hs, ht, rowacc, abc_d, cacc_d, cacc_g, cacc_u,
+    bv_d, rd, cd, rg, cg, ru, cu, rbuf_d, rbuf_g, rbuf_u, cbuf_d, cbuf_g, cbuf_u, sbuf, sacc, wacc,
     sem, r_send, r_recv, c_send, c_recv, s_send, s_recv,
 ):
     G, W = (gd, gg, gu), (wd, wg, wu)
@@ -415,7 +416,7 @@
     all_tiles(DOWN).wait_recv()
     run(update_units(DOWN))
     all_tiles(GATE).wait_recv()
-    run(update_units(GATE))
+    kap[GATE] = step_of(GATE, sbuf.at[GATE], rel[0], clip[0])
     row_copy(UP).wait_send()
     all_cols(UP).wait_send()
     all_cols(EARLY).wait_send()
@@ -425,28 +426,35 @@
 
 
 def update_kernel(
-    gu, wu, wd, wg, rd, cd, rg, cg, ru, cu, kap, abc, bv,
-    wu_o, wd_o, wg_o, rd_o, cd_o, rg_o, cg_o, ru_o, cu_o, stage, sem,
+    gu, wu, wd, wg, rd, cd, rg, cg, ru, cu, kap, abc_u, bv_u, gg, abc_g, bv_g,
+    wu_o, wd_o, wg_o, rd_o, cd_o, rg_o, cg_o, ru_o, cu_o, stage_g, stage_u, sem,
 ):
-    srcs = (wd, wg, rd, cd, rg, cg, ru, cu)
-    dsts = (wd_o, wg_o, rd_o, cd_o, rg_o, cg_o, ru_o, cu_o)
-    copies = [pltpu.make_async_copy(src, dst, sem) for src, dst in zip(srcs, dsts)]
-    for c in copies:
-        c.start()
-    m, n = SHAPES[UP]
-    k = kap[UP, 0:1, :]
-    for r in range(0, m, CHUNK):
-        ka = abc[r:r + CHUNK, :] * k
-        for t in range(n // LANES):
-            cols = slice(t * LANES, (t + 1) * LANES)
-            stage[r:r + CHUNK, cols] = wu[r:r + CHUNK, cols] - gu[r:r + CHUNK, cols] * ka * bv[t:t + 1, :]
-        copies.append(pltpu.make_async_copy(stage.at[r:r + CHUNK, :], wu_o.at[r:r + CHUNK, :], sem))
+    copies = []
+
+    def write(src, dst):
+        copies.append(pltpu.make_async_copy(src, dst, sem))
         copies[-1].start()
+
+    write(wd, wd_o)
+    for src, dst in ((rd, rd_o), (cd, cd_o), (rg, rg_o), (cg, cg_o), (ru, ru_o), (cu, cu_o)):
+        write(src, dst)
+    for mat, g, w, abc, bv, stage, out in (
+        (GATE, gg, wg, abc_g, bv_g, stage_g, wg_o), (UP, gu, wu, abc_u, bv_u, stage_u, wu_o),
+    ):
+        m, n = SHAPES[mat]
+        k = kap[mat, 0:1, :]
+        for r in range(0, m, CHUNK):
+            rows = slice(r, r + CHUNK)
+            ka = abc[rows, :] * k
+            for t in range(n // LANES):
+                cols = slice(t * LANES, (t + 1) * LANES)
+                stage[rows, cols] = w[rows, cols] - g[rows, cols] * ka * bv[t:t + 1, :]
+            write(stage.at[rows, :], out.at[rows, :])
     for copy in copies:
         copy.wait()
 
 
-VMEM_LIMIT = 41 * 1024 * 1024
+VMEM_LIMIT = 36900000
 
 
 def local_program(x_in, h_act, d_gate, d_up, d_out, w_gate, w_up, w_down, r_gate, c_gate, r_up, c_up, r_down, c_down, beta_two, rel_step, clip_thr):
@@ -468,22 +476,21 @@
         main_kernel,
         out_shape=[pltpu.VMEM(SHAPES[UP], F32)] * 2 + [pltpu.VMEM(s, F32) for s in SHAPES[:2]]
         + [pltpu.VMEM(s, F32) for s in stat_pairs]
-        + [pltpu.VMEM((3, 8, LANES), F32), pltpu.VMEM((512, LANES), F32), pltpu.VMEM(cols[UP], F32)],
+        + [pltpu.VMEM((3, 8, LANES), F32), pltpu.VMEM((512, LANES), F32), pltpu.VMEM(cols[UP], F32)]
+        + [pltpu.VMEM(SHAPES[GATE], F32), pltpu.VMEM((512, LANES), F32), pltpu.VMEM(cols[GATE], F32)],
         in_specs=[any_spec] * 14 + [smem_spec] * 3,
-        out_specs=[vmem_spec] * 13,
+        out_specs=[vmem_spec] * 16,
         scratch_shapes=[
             pltpu.VMEM(SHAPES[DOWN], F32),
-            pltpu.VMEM(SHAPES[GATE], F32),
             pltpu.VMEM((3, K, 1024), BF16),
             pltpu.VMEM((512, K), BF16),
             pltpu.VMEM((K, 1408), BF16),
             pltpu.VMEM((1408, K), BF16),
             pltpu.VMEM((1408, LANES), F32),
             pltpu.VMEM((1408, LANES), F32),
-            pltpu.VMEM((512, LANES), F32),
         ]
         + [pltpu.VMEM((8, n), F32) for m, n in SHAPES]
-        + [pltpu.VMEM(s, F32) for s in cols[:2]]
+        + [pltpu.VMEM(cols[DOWN], F32)]
         + [pltpu.VMEM(s, F32) for s in stat_pairs]
         + [pltpu.VMEM((COLS, *s), F32) for s in rows]
         + [pltpu.VMEM((ROWS, *s), F32) for s in cols]
@@ -504,9 +511,9 @@
     res = pl.pallas_call(
         update_kernel,
         out_shape=[jax.ShapeDtypeStruct(s, F32) for s in (SHAPES[UP], *SHAPES[:2], *stat_pairs)],
-        in_specs=[vmem_spec] * 13,
+        in_specs=[vmem_spec] * 16,
         out_specs=[any_spec] * 9,
-        scratch_shapes=[pltpu.VMEM(SHAPES[UP], F32), dma],
+        scratch_shapes=[pltpu.VMEM(SHAPES[GATE], F32), pltpu.VMEM(SHAPES[UP], F32), dma],
         compiler_params=pltpu.CompilerParams(vmem_limit_bytes=VMEM_LIMIT),
         name="update",
     )(*held)

time: 41 us -> 41.2 us (level)
  no operation moved by 1% of the time
where the time goes in v8:
time: 41.2 us; the launch traced here: 41 us
  Pallas kernels  38.3 us (93%)
  between operations  2.75 us (7%)
    pallas_call x1, Pallas kernels, local_program(): pl.pallas_call(main_kernel, out_shape=[pltpu.VMEM(SHAPES[UP], F32)] * 2 +...  32.2 us
    pallas_call x1, Pallas kernels, local_program(): pl.pallas_call(update_kernel, out_shape=[jax.ShapeDtypeStruct(s, F32) for...  6.04 us

profile of v8, /device:TPU:0, one launch (start us, length us, event | category | flops | bytes accessed | tf_op | source)
XLA Modules:
  0.0 41.0 jit_solution(8962375226619578958)
XLA Ops:
  2.6 32.2 %main.1 = (f32[512,2816]{1,0:T(8,128)S(1)}, f32[512,2816]{1,0:T(8,128)S(1)}, f32[1408,1024]{1,0:T(8,128)S(1)}, f32[512,2816]{1,0:T(8,128)S(1)}, f32[11,128]{1,0:...) custom-call(bf16[2048,512]{1,0:T(8,128)(2,1)} %x_hbm.1, ...), custom_call_target="tpu_custom_call" | custom-call | tf_op jit(solution)/shard_map/main/pallas_call | solution.py:475
  34.8 6.0 %update.1 = (f32[512,2816]{1,0:T(8,128)}, f32[1408,1024]{1,0:T(8,128)}, f32[512,2816]{1,0:T(8,128)}, f32[11,128]{1,0:T(8,128)}, f32[8,128]{1,0:T(8,128)}, /*inde...) custom-call(f32[512,2816]{1,0:T(8,128)S(1)} %get-tuple-element.34.gu, ...), custom_call_target="tpu_custom_call" | custom-call | tf_op jit(solution)/shard_map/update/pallas_call | solution.py:511
